TPU v7x, 256 devices: a whole 4x4x8 slice. The times are simulated.
256 devices in a mesh: stream: 32 (over y_hi, z, core), tm: 8 (over x, y_lo).
Axes of the slice: x: 4, y: 4 (y_hi: 2, y_lo: 2; y = y_hi * 2 + y_lo), z: 8, core: 2. Of those that a mesh axis runs over, the one named last changes fastest.
Arguments:
- signal: bfloat16 [64, 2, 4194304], P('stream', None, 'tm'), parts along dimension 0, may hold values from -11 to 11
- taps: float32 [16, 4096], replicated, may hold values from -1.5 to 1.5
Outputs:
- channels_out: float32 [64, 2, 4096, 1024], P('stream', None, 'tm'), parts along dimension 0
There are 32 independent parts, one for each index of `stream`. A program takes and returns all parts, laid end to end along the dimension named above; an argument that names none is the same for every part. Nothing has to cross between parts.
All inputs are finite; a program needn't handle non-finite values.
Results may differ from a plain program's by a relative error of at most 0.0003.
Values may be sent and summed in bfloat16 or wider, within the bound.
No kernel may reach another device: no remote copies, remote signals or barrier semaphores. Data moves between devices by JAX's collectives and lax.ppermute only.
A program may use at most 128 MiB of HBM per device.

v0:
```python
import math

import jax
import jax.numpy as jnp
import numpy as np
from jax import lax
from jax.experimental import pallas as pl
from jax.experimental.pallas import tpu as pltpu
from jax.sharding import PartitionSpec as P


SLOW = 32
LANES = 128
TURN = 16
LEAD = 16
PAIR = 2
UNROLL = 4
PITCH = 36
POWER = 12
FLOOR = 2.0**-10.25
REACH = 2.0**10.25


def tables(channels):
    slow = np.arange(SLOW)[:, None]
    fast = np.arange(LANES)[None, :]
    angle = -2.0 * math.pi * slow * fast / channels
    twist = np.stack([np.cos(angle), np.sin(angle)]).astype(np.float32)
    turn = 2.0 * math.pi * (np.arange(LANES)[:, None] * fast % LANES) / LANES
    cosine, sine = np.cos(turn), np.sin(turn)
    matrix = np.block([[cosine, sine], [-sine, cosine]]) / math.sqrt(channels)
    high = matrix.astype(jnp.bfloat16)
    low = (matrix - high.astype(np.float64)).astype(jnp.bfloat16)
    return twist, np.concatenate([high, low, high], axis=1)


def turned(value, numerator, denominator):
    real, imag = value
    eighth = (8 * numerator) % (8 * denominator)
    if eighth % denominator == 0:
        step = eighth // denominator
        half = math.sqrt(0.5)
        return [
            lambda: (real, imag),
            lambda: ((real + imag) * half, (imag - real) * half),
            lambda: (imag, -real),
            lambda: ((imag - real) * half, (real + imag) * -half),
            lambda: (-real, -imag),
            lambda: ((real + imag) * -half, (real - imag) * half),
            lambda: (-imag, real),
            lambda: ((real - imag) * half, (real + imag) * half),
        ][step]()
    angle = -2.0 * math.pi * numerator / denominator
    cosine, sine = math.cos(angle), math.sin(angle)
    return (real * cosine - imag * sine, real * sine + imag * cosine)


def fourier(values):
    count = len(values)
    if count == 1:
        return values
    even = fourier(values[0::2])
    odd = fourier(values[1::2])
    odd = [turned(item, index, count) for index, item in enumerate(odd)]
    upper = [(a[0] + b[0], a[1] + b[1]) for a, b in zip(even, odd)]
    lower = [(a[0] - b[0], a[1] - b[1]) for a, b in zip(even, odd)]
    return upper + lower


def filter_kernel(frames, taps, grid, largest, window):
    depth = taps.shape[0]
    count = frames.shape[1]
    window[pl.ds(0, LEAD), :] = jnp.zeros((LEAD, LANES), jnp.float32)

    def step(number, most):
        part = number // SLOW
        slow = number % SLOW
        columns = pl.ds(pl.multiple_of(slow * LANES, LANES), LANES)
        window[pl.ds(LEAD, count), :] = frames[part, :, columns].astype(jnp.float32)
        weights = [taps[pl.ds(k, 1), columns] for k in range(depth)]
        for block in range(count // 8):
            total = None
            for k in range(depth):
                if 8 * block + 7 < k:
                    continue
                term = weights[k] * window[pl.ds(LEAD + block * 8 - k, 8), :]
                total = term if total is None else total + term
            grid[part, slow, pl.ds(block * 8, 8), :] = total
            most = jnp.maximum(most, jnp.abs(total))
        return most

    largest[...] = lax.fori_loop(0, 2 * SLOW, step, jnp.zeros((8, LANES), jnp.float32))


def filtered(frames, taps):
    count = frames.shape[1]
    whole = pl.BlockSpec(memory_space=pltpu.VMEM)
    return pl.pallas_call(
        filter_kernel,
        out_shape=[
            jax.ShapeDtypeStruct((2, SLOW, count, LANES), jnp.float32),
            jax.ShapeDtypeStruct((8, LANES), jnp.float32),
        ],
        in_specs=[whole] * 2,
        out_specs=[whole] * 2,
        scratch_shapes=[pltpu.VMEM((LEAD + count, LANES), jnp.float32)],
        compiler_params=pltpu.CompilerParams(vmem_limit_bytes=12 * 1024 * 1024),
        name="filter",
    )(frames, taps)


def encode_kernel(place, edge, taps, grid, largest, twist, matrix, *rest):
    pieces = rest[:8]
    window, head, half, split_high, split_low, rows = rest[8:]
    depth = taps.shape[0]
    count = grid.shape[2]
    me = place[0]
    window[pl.ds(LEAD, LEAD), :] = jnp.zeros((LEAD, LANES), jnp.float32)

    def head_step(number, most):
        part = number // SLOW
        slow = number % SLOW
        columns = pl.ds(pl.multiple_of(slow * LANES, LANES), LANES)
        window[pl.ds(0, LEAD), :] = edge[part, :, columns].astype(jnp.float32)
        weights = [taps[pl.ds(k, 1), columns] for k in range(depth)]
        for block in range(LEAD // 8):
            times = pl.ds(block * 8, 8)
            total = grid[part, slow, times, :]
            for k in range(8 * block + 1, depth):
                total = total + weights[k] * window[pl.ds(LEAD + block * 8 - k, 8), :]
            head[part, slow, times, :] = total
            most = jnp.maximum(most, jnp.abs(total))
        return most

    most = lax.fori_loop(0, 2 * SLOW, head_step, largest[...], unroll=4)
    bound = jnp.max(most) * math.sqrt(2.0 * LANES * SLOW)
    scale = jnp.full((8, LANES), REACH, jnp.float32) / jnp.maximum(bound, 1e-35)
    scale = scale.astype(jnp.bfloat16).astype(jnp.float32)

    def slow_block(source, times):
        for j in range(4):
            column = [(source[0, 4 * i + j, times, :], source[1, 4 * i + j, times, :]) for i in range(8)]
            for u, item in enumerate(fourier(column)):
                real, imag = turned(item, j * u, SLOW)
                half[0, 4 * u + j] = real
                half[1, 4 * u + j] = imag
        for u in range(8):
            column = [(half[0, 4 * u + j], half[1, 4 * u + j]) for j in range(4)]
            for w, (real, imag) in enumerate(fourier(column)):
                slow = u + 8 * w
                cosine = twist[0, pl.ds(slow, 1), :]
                sine = twist[1, pl.ds(slow, 1), :]
                for part, value in enumerate((real * cosine - imag * sine, real * sine + imag * cosine)):
                    top = value.astype(jnp.bfloat16)
                    lanes = pl.ds(part * LANES, LANES)
                    split_high[slow, times, lanes] = top
                    split_low[slow, times, lanes] = (value - top.astype(jnp.float32)).astype(jnp.bfloat16)

    def slow_step(block, carry):
        slow_block(grid, pl.ds(pl.multiple_of(block * TURN, TURN), TURN))
        return carry

    slow_block(head, pl.ds(0, TURN))
    lax.fori_loop(1, count // TURN, slow_step, 0)

    def fast_step(number, carry):
        near = split_high[pl.ds(number * PAIR, PAIR)].reshape(PAIR * count, 2 * LANES)
        far = split_low[pl.ds(number * PAIR, PAIR)].reshape(PAIR * count, 2 * LANES)
        both = jnp.concatenate([near, near, far], axis=1)
        value = lax.dot_general(
            matrix[...], both, (((1,), (1,)), ((), ())), preferred_element_type=jnp.float32
        )
        level = jnp.abs(value) * scale[:1, :1] + FLOOR
        square = level * level
        sixth = square * level
        sixth = sixth * sixth
        level = sixth * sixth
        level = jnp.where(value < 0.0, -level, level)
        for part in range(2):
            for item in range(PAIR):
                rows[part, pl.ds(number * PAIR + item, LANES, stride=PITCH), :] = level[
                    part * LANES : (part + 1) * LANES, item * count : (item + 1) * count
                ]
        return carry

    lax.fori_loop(0, SLOW // PAIR, fast_step, 0, unroll=UNROLL)

    share = LANES // 8
    for d in range(8):
        first = jnp.bitwise_xor(me, d) * share * PITCH
        for part in range(2):
            for fast in range(share):
                start = pl.multiple_of(first + fast * PITCH, 4)
                pieces[d][pl.ds((part * share + fast) * SLOW, SLOW), :] = rows[
                    part, pl.ds(start, SLOW), :
                ].astype(jnp.bfloat16)
        pieces[d][pl.ds(2 * share * SLOW, 16), :] = jnp.concatenate([scale, scale], axis=0).astype(jnp.bfloat16)


def encode(place, edge, taps, grid, largest, twist, matrix):
    count = grid.shape[2]
    channels = taps.shape[1]
    piece = jax.ShapeDtypeStruct((2 * channels // 8 + 16, count), jnp.bfloat16)
    whole = pl.BlockSpec(memory_space=pltpu.VMEM)
    return pl.pallas_call(
        encode_kernel,
        out_shape=[piece] * 8,
        in_specs=[pl.BlockSpec(memory_space=pltpu.SMEM)] + [whole] * 6,
        out_specs=[whole] * 8,
        scratch_shapes=[
            pltpu.VMEM((2 * LEAD, LANES), jnp.float32),
            pltpu.VMEM((2, SLOW, LEAD, LANES), jnp.float32),
            pltpu.VMEM((2, SLOW, TURN, LANES), jnp.float32),
            pltpu.VMEM((SLOW, count, 2 * LANES), jnp.bfloat16),
            pltpu.VMEM((SLOW, count, 2 * LANES), jnp.bfloat16),
            pltpu.VMEM((2, PITCH * LANES, LANES), jnp.float32),
        ],
        compiler_params=pltpu.CompilerParams(vmem_limit_bytes=20 * 1024 * 1024),
        name="encode",
    )(place, edge, taps, grid, largest, twist, matrix)


def decode_kernel(place, *rest):
    pieces = rest[:8]
    output = rest[-1]
    width = output.shape[2]
    half = (pieces[0].shape[0] - 16) // 2
    me = place[0]
    base = pl.program_id(0) * width
    inverse = [1.0 / pieces[d][pl.ds(2 * half, 16), :].astype(jnp.float32) for d in range(8)]

    def step(number, carry):
        power = None
        found = []
        for d in range(8):
            for part in range(2):
                start = pl.multiple_of(part * half + base + number * 16, 16)
                code = pieces[d][pl.ds(start, 16), :].astype(jnp.float32)
                level = jnp.exp2(jnp.log2(jnp.abs(code)) * (1.0 / POWER)) - FLOOR
                level = level * inverse[d]
                found.append(jnp.where(code < 0.0, -level, level))
                power = level * level if power is None else power + level * level
        total = jnp.sum(power, axis=1, keepdims=True)
        factor = lax.rsqrt(total / (8 * LANES) + 1.0)
        for d in range(8):
            lanes = pl.ds(pl.multiple_of(jnp.bitwise_xor(me, d) * LANES, LANES), LANES)
            for part in range(2):
                output[0, part, pl.ds(pl.multiple_of(number * 16, 16), 16), lanes] = found[2 * d + part] * factor
        return carry

    lax.fori_loop(0, width // 16, step, 0, unroll=4)


def decode(place, pieces, stream, streams, before):
    half = (pieces[0].shape[0] - 16) // 2
    blocks = 4
    shape = (streams, 2, half, 8 * LANES)
    whole = pl.BlockSpec(memory_space=pltpu.VMEM)
    operands = [place, *pieces]
    in_specs = [pl.BlockSpec(memory_space=pltpu.SMEM)] + [whole] * 8
    aliases = {}
    if before is not None:
        operands.append(before)
        in_specs.append(pl.BlockSpec(memory_space=pl.ANY))
        aliases = {9: 0}
    return pl.pallas_call(
        decode_kernel,
        grid=(blocks,),
        out_shape=jax.ShapeDtypeStruct(shape, jnp.float32),
        in_specs=in_specs,
        out_specs=pl.BlockSpec((1, 2, half // blocks, 8 * LANES), lambda i: (stream, 0, i, 0)),
        input_output_aliases=aliases,
        compiler_params=pltpu.CompilerParams(vmem_limit_bytes=16 * 1024 * 1024),
        name="decode",
    )(*operands)


def shards(signal, taps):
    streams = signal.shape[0]
    channels = taps.shape[1]
    count = signal.shape[2] // channels
    size = lax.axis_size("tm")
    place = lax.axis_index("tm").astype(jnp.int32)[None]
    twist, matrix = tables(channels)
    route = [(i, i + 1) for i in range(size - 1)]
    tail = signal[:, :, (count - LEAD) * channels :]
    edges = [lax.ppermute(tail[stream], "tm", route) for stream in range(streams)]
    arrived = []
    held = signal
    for stream in range(streams):
        frames = held[stream].reshape(2, count, channels)
        grid, largest = filtered(frames, taps)
        edge = edges[stream].reshape(2, LEAD, channels)
        pieces = list(encode(place, edge, taps, grid, largest, twist, matrix))
        held, pieces[0] = lax.optimization_barrier((held, pieces[0]))
        for d in range(1, size):
            pieces[d] = lax.ppermute(pieces[d], "tm", [(i, i ^ d) for i in range(size)])
        arrived.append(pieces)
    output = None
    for stream in range(streams):
        output = decode(place, arrived[stream], stream, streams, output)
    return output


def solution(mesh):
    in_specs = (P("stream", None, "tm"), P())
    out_specs = P("stream", None, "tm", None)
    return jax.shard_map(shards, mesh=mesh, in_specs=in_specs, out_specs=out_specs, check_vma=False)
```

profile of v0, /device:TPU:192, one launch (start us, length us, event | category | flops | bytes accessed | tf_op | source)
XLA Modules:
  0.0 104.9 jit_solution(16058986087855237235)
XLA Ops:
  0.0 2.2 %slice_bitcast_fusion = (bf16[2,65536]{1,0:T(2,128)(2,1)S(1)}, bf16[2,65536]{1,0:T(2,128)(2,1)}) fusion(bf16[2,2,524288]{2,1,0:T(2,128)(2,1)} %param.4), kind=kLoop, calls=%fused_computation.4 | loop fusion | bytes 1048576 | tf_op jit(solution)/shard_map/squeeze | solution.py:287
  2.2 3.5 %collective-permute-start = (bf16[2,65536]{1,0:T(2,128)(2,1)}, bf16[2,65536]{1,0:T(2,128)(2,1)S(1)}, u32[]{:S(2)}, u32[]{:S(2)}) collective-permute-start(bf16[2,65536]{1,0:T(2,128)(2,1)} %get-tuple-element.52), channel_id=1, source_target_pairs={{0,1},{1,2},{2,3},{3,4},{4,5},{5,6},{6,7},{8,9},{9,10},{10,11},{11... | collective-permute-start | bytes 786440 | tf_op jit(solution)/shard_map/ppermute | solution.py:287
  5.7 0.0 copy-start
  5.7 0.0 copy-start.1
  5.8 0.0 copy-start.2
  5.8 1.3 %copy.15 = bf16[1,2,128,4096]{3,2,1,0:T(8,128)(2,1)S(1)} copy(bf16[1,2,128,4096]{3,1,2,0:T(2,128)(2,1)S(1)} %bitcast.27) | data formatting | bytes 4194304
  7.1 0.0 copy-done
  7.1 5.8 %filter.2 = (f32[2,32,128,128]{3,2,1,0:T(8,128)S(1)}, f32[8,128]{1,0:T(8,128)S(1)}) custom-call(bf16[2,128,4096]{2,1,0:T(8,128)(2,1)S(1)} %bitcast.23, f32[16,4096]{1,0:T(8,128)S(1)} %copy-done), custom_call_target="tpu_custom_call" | custom-call | tf_op jit(solution)/shard_map/filter/pallas_call | solution.py:98
  12.9 0.0 collective-permute-done
  12.9 0.2 copy.17
  13.1 0.0 slice-start.1
  13.1 6.5 %encode.2 = (bf16[1040,128]{1,0:T(8,128)(2,1)S(1)}, bf16[1040,128]{1,0:T(8,128)(2,1)S(1)}, bf16[1040,128]{1,0:T(8,128)(2,1)S(1)}, bf16[1040,128]{1,0:T(8,128)(2,...) custom-call(s32[1]{0:T(128)} %bitcast.place, ...), custom_call_target="tpu_custom_call" | custom-call | tf_op jit(solution)/shard_map/encode/pallas_call | solution.py:205
  19.6 1.4 %collective-permute-start.9 = (bf16[1040,128]{1,0:T(8,128)(2,1)S(1)}, bf16[1040,128]{1,0:T(8,128)(2,1)S(1)}, u32[]{:S(2)}, u32[]{:S(2)}) collective-permute-start(bf16[1040,128]{1,0:T(8,128)(2,1)S(1)} %get-tuple-element.44), channel_id=1, source_target_pairs={{0,1},{1,0},{2,3},{3,2},{4,5},{5,4},{6,7},{7,6},{8,9},{9,8},{10,11... | collective-permute-start | bytes 798728 | tf_op jit(solution)/shard_map/ppermute | solution.py:297
  21.0 1.5 %collective-permute-start.10 = (bf16[1040,128]{1,0:T(8,128)(2,1)S(1)}, bf16[1040,128]{1,0:T(8,128)(2,1)S(1)}, u32[]{:S(2)}, u32[]{:S(2)}) collective-permute-start(bf16[1040,128]{1,0:T(8,128)(2,1)S(1)} %get-tuple-element.45), channel_id=1, source_target_pairs={{0,2},{1,3},{2,0},{3,1},{4,6},{5,7},{6,4},{7,5},{8,10},{9,11},{10,... | collective-permute-start | bytes 798728 | tf_op jit(solution)/shard_map/ppermute | solution.py:297
  22.5 0.6 collective-permute-start.11
  23.2 3.4 %collective-permute-start.12 = (bf16[1040,128]{1,0:T(8,128)(2,1)S(1)}, bf16[1040,128]{1,0:T(8,128)(2,1)S(1)}, u32[]{:S(2)}, u32[]{:S(2)}) collective-permute-start(bf16[1040,128]{1,0:T(8,128)(2,1)S(1)} %get-tuple-element.47), channel_id=1, source_target_pairs={{0,4},{1,5},{2,6},{3,7},{4,0},{5,1},{6,2},{7,3},{8,12},{9,13},{10,... | collective-permute-start | bytes 798728 | tf_op jit(solution)/shard_map/ppermute | solution.py:297
  26.6 2.6 %collective-permute-start.1 = (bf16[2,65536]{1,0:T(2,128)(2,1)S(1)}, bf16[2,65536]{1,0:T(2,128)(2,1)S(1)}, u32[]{:S(2)}, u32[]{:S(2)}) collective-permute-start(bf16[2,65536]{1,0:T(2,128)(2,1)S(1)} %get-tuple-element.51), channel_id=1, source_target_pairs={{0,1},{1,2},{2,3},{3,4},{4,5},{5,6},{6,7},{8,9},{9,10},{10,11},{11... | collective-permute-start | bytes 786440 | tf_op jit(solution)/shard_map/ppermute | solution.py:287
  29.2 8.9 %collective-permute-done.1 = bf16[2,65536]{1,0:T(2,128)(2,1)S(1)} collective-permute-done((bf16[2,65536]{1,0:T(2,128)(2,1)S(1)}, bf16[2,65536]{1,0:T(2,128)(2,1)S(1)}, u32[]{:S(2)}, u32[]{:S(2)}) %collective-permute-start.1) | collective-permute-done | bytes 262176 | tf_op jit(solution)/shard_map/ppermute | solution.py:287
  38.1 0.1 copy.16
  38.3 10.8 %collective-permute-start.13 = (bf16[1040,128]{1,0:T(8,128)(2,1)S(1)}, bf16[1040,128]{1,0:T(8,128)(2,1)S(1)}, u32[]{:S(2)}, u32[]{:S(2)}) collective-permute-start(bf16[1040,128]{1,0:T(8,128)(2,1)S(1)} %get-tuple-element.48), channel_id=1, source_target_pairs={{0,5},{1,4},{2,7},{3,6},{4,1},{5,0},{6,3},{7,2},{8,13},{9,12},{10,... | collective-permute-start | bytes 798728 | tf_op jit(solution)/shard_map/ppermute | solution.py:297
  49.1 1.3 %copy.14 = bf16[1,2,128,4096]{3,2,1,0:T(8,128)(2,1)S(1)} copy(bf16[1,2,128,4096]{3,1,2,0:T(2,128)(2,1)S(1)} %bitcast.28) | data formatting | bytes 4194304
  50.4 5.8 %filter.3 = (f32[2,32,128,128]{3,2,1,0:T(8,128)S(1)}, f32[8,128]{1,0:T(8,128)S(1)}) custom-call(bf16[2,128,4096]{2,1,0:T(8,128)(2,1)S(1)} %bitcast.24, f32[16,4096]{1,0:T(8,128)S(1)} %copy-done), custom_call_target="tpu_custom_call" | custom-call | tf_op jit(solution)/shard_map/filter/pallas_call | solution.py:98
  56.1 6.5 %encode.3 = (bf16[1040,128]{1,0:T(8,128)(2,1)S(1)}, bf16[1040,128]{1,0:T(8,128)(2,1)S(1)}, bf16[1040,128]{1,0:T(8,128)(2,1)S(1)}, bf16[1040,128]{1,0:T(8,128)(2,...) custom-call(s32[1]{0:T(128)} %bitcast.place, ...), custom_call_target="tpu_custom_call" | custom-call | tf_op jit(solution)/shard_map/encode/pallas_call | solution.py:205
  62.7 0.0 collective-permute-done.9.rest_1_
  62.7 1.1 %collective-permute-start.14 = (bf16[1040,128]{1,0:T(8,128)(2,1)S(1)}, bf16[1040,128]{1,0:T(8,128)(2,1)S(1)}, u32[]{:S(2)}, u32[]{:S(2)}) collective-permute-start(bf16[1040,128]{1,0:T(8,128)(2,1)S(1)} %get-tuple-element.49), channel_id=1, source_target_pairs={{0,6},{1,7},{2,4},{3,5},{4,2},{5,3},{6,0},{7,1},{8,14},{9,15},{10,... | collective-permute-start | bytes 798728 | tf_op jit(solution)/shard_map/ppermute | solution.py:297
  63.8 0.0 collective-permute-done.10.rest_2_
  63.8 2.4 %collective-permute-start.15 = (bf16[1040,128]{1,0:T(8,128)(2,1)S(1)}, bf16[1040,128]{1,0:T(8,128)(2,1)S(1)}, u32[]{:S(2)}, u32[]{:S(2)}) collective-permute-start(bf16[1040,128]{1,0:T(8,128)(2,1)S(1)} %get-tuple-element.50), channel_id=1, source_target_pairs={{0,7},{1,6},{2,5},{3,4},{4,3},{5,2},{6,1},{7,0},{8,15},{9,14},{10,... | collective-permute-start | bytes 798728 | tf_op jit(solution)/shard_map/ppermute | solution.py:297
  66.2 0.0 collective-permute-done.11.rest_3_
  66.2 1.3 %collective-permute-start.2 = (bf16[1040,128]{1,0:T(8,128)(2,1)S(1)}, bf16[1040,128]{1,0:T(8,128)(2,1)S(1)}, u32[]{:S(2)}, u32[]{:S(2)}) collective-permute-start(bf16[1040,128]{1,0:T(8,128)(2,1)S(1)} %get-tuple-element.36), channel_id=1, source_target_pairs={{0,1},{1,0},{2,3},{3,2},{4,5},{5,4},{6,7},{7,6},{8,9},{9,8},{10,11... | collective-permute-start | bytes 798728 | tf_op jit(solution)/shard_map/ppermute | solution.py:297
  67.5 0.0 collective-permute-done.12.rest_4_
  67.5 0.2 collective-permute-start.3
  67.7 0.0 collective-permute-done.13.rest_5_
  67.7 2.0 %collective-permute-start.4 = (bf16[1040,128]{1,0:T(8,128)(2,1)S(1)}, bf16[1040,128]{1,0:T(8,128)(2,1)S(1)}, u32[]{:S(2)}, u32[]{:S(2)}) collective-permute-start(bf16[1040,128]{1,0:T(8,128)(2,1)S(1)} %get-tuple-element.38), channel_id=1, source_target_pairs={{0,3},{1,2},{2,1},{3,0},{4,7},{5,6},{6,5},{7,4},{8,11},{9,10},{10,... | collective-permute-start | bytes 798728 | tf_op jit(solution)/shard_map/ppermute | solution.py:297
  69.7 2.0 %collective-permute-done.14.rest_6_ = bf16[1040,128]{1,0:T(8,128)(2,1)S(1)} collective-permute-done((bf16[1040,128]{1,0:T(8,128)(2,1)S(1)}, bf16[1040,128]{1,0:T(8,128)(2,1)S(1)}, u32[]{:S(2)}, u32[]{:S(2)}) %collective-permute-start.14) | collective-permute-done | bytes 266272 | tf_op jit(solution)/shard_map/ppermute | solution.py:297
  71.7 0.8 collective-permute-start.5
  72.5 2.9 %collective-permute-done.15.rest_7_ = bf16[1040,128]{1,0:T(8,128)(2,1)S(1)} collective-permute-done((bf16[1040,128]{1,0:T(8,128)(2,1)S(1)}, bf16[1040,128]{1,0:T(8,128)(2,1)S(1)}, u32[]{:S(2)}, u32[]{:S(2)}) %collective-permute-start.15) | collective-permute-done | bytes 266272 | tf_op jit(solution)/shard_map/ppermute | solution.py:297
  75.4 2.3 %collective-permute-start.6 = (bf16[1040,128]{1,0:T(8,128)(2,1)S(1)}, bf16[1040,128]{1,0:T(8,128)(2,1)S(1)}, u32[]{:S(2)}, u32[]{:S(2)}) collective-permute-start(bf16[1040,128]{1,0:T(8,128)(2,1)S(1)} %get-tuple-element.40), channel_id=1, source_target_pairs={{0,5},{1,4},{2,7},{3,6},{4,1},{5,0},{6,3},{7,2},{8,13},{9,12},{10,... | collective-permute-start | bytes 798728 | tf_op jit(solution)/shard_map/ppermute | solution.py:297
  77.7 5.3 %collective-permute-done.2.rest_1_ = bf16[1040,128]{1,0:T(8,128)(2,1)S(1)} collective-permute-done((bf16[1040,128]{1,0:T(8,128)(2,1)S(1)}, bf16[1040,128]{1,0:T(8,128)(2,1)S(1)}, u32[]{:S(2)}, u32[]{:S(2)}) %collective-permute-start.2) | collective-permute-done | bytes 266272 | tf_op jit(solution)/shard_map/ppermute | solution.py:297
  82.9 4.8 %collective-permute-start.7 = (bf16[1040,128]{1,0:T(8,128)(2,1)S(1)}, bf16[1040,128]{1,0:T(8,128)(2,1)S(1)}, u32[]{:S(2)}, u32[]{:S(2)}) collective-permute-start(bf16[1040,128]{1,0:T(8,128)(2,1)S(1)} %get-tuple-element.41), channel_id=1, source_target_pairs={{0,6},{1,7},{2,4},{3,5},{4,2},{5,3},{6,0},{7,1},{8,14},{9,15},{10,... | collective-permute-start | bytes 798728 | tf_op jit(solution)/shard_map/ppermute | solution.py:297
  87.7 0.0 collective-permute-done.3.rest_2_
  87.7 0.0 collective-permute-start.8
  87.7 3.6 %decode.2.rest_8_ = f32[2,2,512,1024]{3,2,1,0:T(8,128)} custom-call(s32[1]{0:T(128)} %bitcast.place, bf16[1040,128]{1,0:T(8,128)(2,1)S(1)} %get-tuple-element.43.rest_0_, bf16[1040,128]{1,0:T(8,128)(2,1)S(1)} %collective-permute-done.9.rest_1_, bf16[1040,128]{1,0:T(8,128)(2,1)S(1)} %collective-permute-done.10.rest_2_, ...), custom_call_target="tpu_custom_call" | custom-call | tf_op jit(solution)/shard_map/decode/pallas_call | solution.py:266
  91.4 0.0 collective-permute-done.4.rest_3_
  91.4 0.0 collective-permute-done.5.rest_4_
  91.4 0.4 collective-permute-done.6.rest_5_
  91.8 4.4 %collective-permute-done.7.rest_6_ = bf16[1040,128]{1,0:T(8,128)(2,1)S(1)} collective-permute-done((bf16[1040,128]{1,0:T(8,128)(2,1)S(1)}, bf16[1040,128]{1,0:T(8,128)(2,1)S(1)}, u32[]{:S(2)}, u32[]{:S(2)}) %collective-permute-start.7) | collective-permute-done | bytes 266272 | tf_op jit(solution)/shard_map/ppermute | solution.py:297
  96.2 5.1 %collective-permute-done.8.rest_7_ = bf16[1040,128]{1,0:T(8,128)(2,1)S(1)} collective-permute-done((bf16[1040,128]{1,0:T(8,128)(2,1)S(1)}, bf16[1040,128]{1,0:T(8,128)(2,1)S(1)}, u32[]{:S(2)}, u32[]{:S(2)}) %collective-permute-start.8) | collective-permute-done | bytes 266272 | tf_op jit(solution)/shard_map/ppermute | solution.py:297
  101.3 3.6 %decode.3 = f32[2,2,512,1024]{3,2,1,0:T(8,128)} custom-call(s32[1]{0:T(128)} %bitcast.place, bf16[1040,128]{1,0:T(8,128)(2,1)S(1)} %get-tuple-element.35.rest_0_, bf16[1040,128]{1,0:T(8,128)(2,1)S(1)} %collective-permute-done.2.rest_1_, bf16[1040,128]{1,0:T(8,128)(2,1)S(1)} %collective-permute-done.3.rest_2_, ...), custom_call_target="tpu_custom_call", output_to_operand_aliasing={{}: (9, {})} | custom-call | tf_op jit(solution)/shard_map/decode/pallas_call | solution.py:266
  (5 shorter events, 0.0 us)
Async XLA Ops:
  0.0 5.8 %slice-start = ((bf16[2,2,524288]{2,1,0:T(2,128)(2,1)}), bf16[1,2,524288]{2,1,0:T(2,128)(2,1)S(1)}, s32[]{:S(2)}) async-start(bf16[2,2,524288]{2,1,0:T(2,128)(2,1)} %param.4), calls=%async_computation | async-start | bytes 4194304 | tf_op jit(solution)/shard_map/slice | solution.py:291
  2.2 10.6 %collective-permute-start = (bf16[2,65536]{1,0:T(2,128)(2,1)}, bf16[2,65536]{1,0:T(2,128)(2,1)S(1)}, u32[]{:S(2)}, u32[]{:S(2)}) collective-permute-start(bf16[2,65536]{1,0:T(2,128)(2,1)} %get-tuple-element.52), channel_id=1, source_target_pairs={{0,1},{1,2},{2,3},{3,4},{4,5},{5,6},{6,7},{8,9},{9,10},{10,11},{11... | collective-permute-start | bytes 786440 | tf_op jit(solution)/shard_map/ppermute | solution.py:287
  5.7 1.4 %copy-start = (f32[16,4096]{1,0:T(8,128)S(1)}, f32[16,4096]{1,0:T(8,128)}, u32[]{:S(2)}) copy-start(f32[16,4096]{1,0:T(8,128)} %taps.7) | copy-start | bytes 786436
  5.7 7.3 %copy-start.1 = (bf16[256,768]{1,0:T(8,128)(2,1)S(1)}, bf16[256,768]{1,0:T(8,128)(2,1)}, u32[]{:S(2)}) copy-start(bf16[256,768]{1,0:T(8,128)(2,1)} %constant.9.clone.matrix) | copy-start | bytes 1179652
  5.8 7.3 %copy-start.2 = (f32[2,32,128]{2,1,0:T(8,128)S(1)}, f32[2,32,128]{2,1,0:T(8,128)}, u32[]{:S(2)}) copy-start(f32[2,32,128]{2,1,0:T(8,128)} %constant.8.clone.twist) | copy-start | bytes 98308
  13.1 36.0 %slice-start.1 = ((bf16[2,2,524288]{2,1,0:T(2,128)(2,1)}), bf16[1,2,524288]{2,1,0:T(2,128)(2,1)S(1)}, s32[]{:S(2)}) async-start(bf16[2,2,524288]{2,1,0:T(2,128)(2,1)} %param.4), calls=%async_computation.1 | async-start | bytes 4194304 | tf_op jit(solution)/shard_map/slice | solution.py:291
  19.6 43.1 %collective-permute-start.9 = (bf16[1040,128]{1,0:T(8,128)(2,1)S(1)}, bf16[1040,128]{1,0:T(8,128)(2,1)S(1)}, u32[]{:S(2)}, u32[]{:S(2)}) collective-permute-start(bf16[1040,128]{1,0:T(8,128)(2,1)S(1)} %get-tuple-element.44), channel_id=1, source_target_pairs={{0,1},{1,0},{2,3},{3,2},{4,5},{5,4},{6,7},{7,6},{8,9},{9,8},{10,11... | collective-permute-start | bytes 798728 | tf_op jit(solution)/shard_map/ppermute | solution.py:297
  21.0 42.7 %collective-permute-start.10 = (bf16[1040,128]{1,0:T(8,128)(2,1)S(1)}, bf16[1040,128]{1,0:T(8,128)(2,1)S(1)}, u32[]{:S(2)}, u32[]{:S(2)}) collective-permute-start(bf16[1040,128]{1,0:T(8,128)(2,1)S(1)} %get-tuple-element.45), channel_id=1, source_target_pairs={{0,2},{1,3},{2,0},{3,1},{4,6},{5,7},{6,4},{7,5},{8,10},{9,11},{10,... | collective-permute-start | bytes 798728 | tf_op jit(solution)/shard_map/ppermute | solution.py:297
  22.5 43.6 %collective-permute-start.11 = (bf16[1040,128]{1,0:T(8,128)(2,1)S(1)}, bf16[1040,128]{1,0:T(8,128)(2,1)S(1)}, u32[]{:S(2)}, u32[]{:S(2)}) collective-permute-start(bf16[1040,128]{1,0:T(8,128)(2,1)S(1)} %get-tuple-element.46), channel_id=1, source_target_pairs={{0,3},{1,2},{2,1},{3,0},{4,7},{5,6},{6,5},{7,4},{8,11},{9,10},{10,... | collective-permute-start | bytes 798728 | tf_op jit(solution)/shard_map/ppermute | solution.py:297
  23.2 44.3 %collective-permute-start.12 = (bf16[1040,128]{1,0:T(8,128)(2,1)S(1)}, bf16[1040,128]{1,0:T(8,128)(2,1)S(1)}, u32[]{:S(2)}, u32[]{:S(2)}) collective-permute-start(bf16[1040,128]{1,0:T(8,128)(2,1)S(1)} %get-tuple-element.47), channel_id=1, source_target_pairs={{0,4},{1,5},{2,6},{3,7},{4,0},{5,1},{6,2},{7,3},{8,12},{9,13},{10,... | collective-permute-start | bytes 798728 | tf_op jit(solution)/shard_map/ppermute | solution.py:297
  26.6 11.6 %collective-permute-start.1 = (bf16[2,65536]{1,0:T(2,128)(2,1)S(1)}, bf16[2,65536]{1,0:T(2,128)(2,1)S(1)}, u32[]{:S(2)}, u32[]{:S(2)}) collective-permute-start(bf16[2,65536]{1,0:T(2,128)(2,1)S(1)} %get-tuple-element.51), channel_id=1, source_target_pairs={{0,1},{1,2},{2,3},{3,4},{4,5},{5,6},{6,7},{8,9},{9,10},{10,11},{11... | collective-permute-start | bytes 786440 | tf_op jit(solution)/shard_map/ppermute | solution.py:287
  38.3 29.4 %collective-permute-start.13 = (bf16[1040,128]{1,0:T(8,128)(2,1)S(1)}, bf16[1040,128]{1,0:T(8,128)(2,1)S(1)}, u32[]{:S(2)}, u32[]{:S(2)}) collective-permute-start(bf16[1040,128]{1,0:T(8,128)(2,1)S(1)} %get-tuple-element.48), channel_id=1, source_target_pairs={{0,5},{1,4},{2,7},{3,6},{4,1},{5,0},{6,3},{7,2},{8,13},{9,12},{10,... | collective-permute-start | bytes 798728 | tf_op jit(solution)/shard_map/ppermute | solution.py:297
  62.7 9.1 %collective-permute-start.14 = (bf16[1040,128]{1,0:T(8,128)(2,1)S(1)}, bf16[1040,128]{1,0:T(8,128)(2,1)S(1)}, u32[]{:S(2)}, u32[]{:S(2)}) collective-permute-start(bf16[1040,128]{1,0:T(8,128)(2,1)S(1)} %get-tuple-element.49), channel_id=1, source_target_pairs={{0,6},{1,7},{2,4},{3,5},{4,2},{5,3},{6,0},{7,1},{8,14},{9,15},{10,... | collective-permute-start | bytes 798728 | tf_op jit(solution)/shard_map/ppermute | solution.py:297
  63.8 11.6 %collective-permute-start.15 = (bf16[1040,128]{1,0:T(8,128)(2,1)S(1)}, bf16[1040,128]{1,0:T(8,128)(2,1)S(1)}, u32[]{:S(2)}, u32[]{:S(2)}) collective-permute-start(bf16[1040,128]{1,0:T(8,128)(2,1)S(1)} %get-tuple-element.50), channel_id=1, source_target_pairs={{0,7},{1,6},{2,5},{3,4},{4,3},{5,2},{6,1},{7,0},{8,15},{9,14},{10,... | collective-permute-start | bytes 798728 | tf_op jit(solution)/shard_map/ppermute | solution.py:297
  66.2 16.8 %collective-permute-start.2 = (bf16[1040,128]{1,0:T(8,128)(2,1)S(1)}, bf16[1040,128]{1,0:T(8,128)(2,1)S(1)}, u32[]{:S(2)}, u32[]{:S(2)}) collective-permute-start(bf16[1040,128]{1,0:T(8,128)(2,1)S(1)} %get-tuple-element.36), channel_id=1, source_target_pairs={{0,1},{1,0},{2,3},{3,2},{4,5},{5,4},{6,7},{7,6},{8,9},{9,8},{10,11... | collective-permute-start | bytes 798728 | tf_op jit(solution)/shard_map/ppermute | solution.py:297
  67.5 20.3 %collective-permute-start.3 = (bf16[1040,128]{1,0:T(8,128)(2,1)S(1)}, bf16[1040,128]{1,0:T(8,128)(2,1)S(1)}, u32[]{:S(2)}, u32[]{:S(2)}) collective-permute-start(bf16[1040,128]{1,0:T(8,128)(2,1)S(1)} %get-tuple-element.37), channel_id=1, source_target_pairs={{0,2},{1,3},{2,0},{3,1},{4,6},{5,7},{6,4},{7,5},{8,10},{9,11},{10,... | collective-permute-start | bytes 798728 | tf_op jit(solution)/shard_map/ppermute | solution.py:297
  67.7 23.7 %collective-permute-start.4 = (bf16[1040,128]{1,0:T(8,128)(2,1)S(1)}, bf16[1040,128]{1,0:T(8,128)(2,1)S(1)}, u32[]{:S(2)}, u32[]{:S(2)}) collective-permute-start(bf16[1040,128]{1,0:T(8,128)(2,1)S(1)} %get-tuple-element.38), channel_id=1, source_target_pairs={{0,3},{1,2},{2,1},{3,0},{4,7},{5,6},{6,5},{7,4},{8,11},{9,10},{10,... | collective-permute-start | bytes 798728 | tf_op jit(solution)/shard_map/ppermute | solution.py:297
  71.7 19.6 %collective-permute-start.5 = (bf16[1040,128]{1,0:T(8,128)(2,1)S(1)}, bf16[1040,128]{1,0:T(8,128)(2,1)S(1)}, u32[]{:S(2)}, u32[]{:S(2)}) collective-permute-start(bf16[1040,128]{1,0:T(8,128)(2,1)S(1)} %get-tuple-element.39), channel_id=1, source_target_pairs={{0,4},{1,5},{2,6},{3,7},{4,0},{5,1},{6,2},{7,3},{8,12},{9,13},{10,... | collective-permute-start | bytes 798728 | tf_op jit(solution)/shard_map/ppermute | solution.py:297
  75.4 16.4 %collective-permute-start.6 = (bf16[1040,128]{1,0:T(8,128)(2,1)S(1)}, bf16[1040,128]{1,0:T(8,128)(2,1)S(1)}, u32[]{:S(2)}, u32[]{:S(2)}) collective-permute-start(bf16[1040,128]{1,0:T(8,128)(2,1)S(1)} %get-tuple-element.40), channel_id=1, source_target_pairs={{0,5},{1,4},{2,7},{3,6},{4,1},{5,0},{6,3},{7,2},{8,13},{9,12},{10,... | collective-permute-start | bytes 798728 | tf_op jit(solution)/shard_map/ppermute | solution.py:297
  82.9 13.3 %collective-permute-start.7 = (bf16[1040,128]{1,0:T(8,128)(2,1)S(1)}, bf16[1040,128]{1,0:T(8,128)(2,1)S(1)}, u32[]{:S(2)}, u32[]{:S(2)}) collective-permute-start(bf16[1040,128]{1,0:T(8,128)(2,1)S(1)} %get-tuple-element.41), channel_id=1, source_target_pairs={{0,6},{1,7},{2,4},{3,5},{4,2},{5,3},{6,0},{7,1},{8,14},{9,15},{10,... | collective-permute-start | bytes 798728 | tf_op jit(solution)/shard_map/ppermute | solution.py:297
  87.7 13.6 %collective-permute-start.8 = (bf16[1040,128]{1,0:T(8,128)(2,1)S(1)}, bf16[1040,128]{1,0:T(8,128)(2,1)S(1)}, u32[]{:S(2)}, u32[]{:S(2)}) collective-permute-start(bf16[1040,128]{1,0:T(8,128)(2,1)S(1)} %get-tuple-element.42), channel_id=1, source_target_pairs={{0,7},{1,6},{2,5},{3,4},{4,3},{5,2},{6,1},{7,0},{8,15},{9,14},{10,... | collective-permute-start | bytes 798728 | tf_op jit(solution)/shard_map/ppermute | solution.py:297
where the time goes:
time: 105 us
  starting transfers between devices  38.7 us (37%)
  Pallas kernels  31.8 us (30%)
  waiting for transfers between devices  29.1 us (28%)
  local copies, waits for them, and re-layouts  5.23 us (5%)
    ppermute x14, starting transfers between devices, shards(): pieces[d] = lax.ppermute(pieces[d], 'tm', [(i, i ^ d) for i in range(size)])  32.6 us
    ppermute x14, waiting for transfers between devices, shards(): pieces[d] = lax.ppermute(pieces[d], 'tm', [(i, i ^ d) for i in range(size)])  20.1 us
    pallas_call x2, Pallas kernels, encode(): pl.pallas_call(encode_kernel, out_shape=[piece] * 8, in_specs=[pl.BlockSp...  13 us
    pallas_call x2, Pallas kernels, filtered(): pl.pallas_call(filter_kernel, out_shape=[jax.ShapeDtypeStruct((2, SLOW, c...  11.5 us
    ppermute x2, waiting for transfers between devices, shards(): lax.ppermute(tail[stream], 'tm', route)  8.95 us
    pallas_call x2, Pallas kernels, decode(): pl.pallas_call(decode_kernel, grid=(blocks,), out_shape=jax.ShapeDtypeStr...  7.25 us
    ppermute x2, starting transfers between devices, shards(): lax.ppermute(tail[stream], 'tm', route)  6.08 us
    unnamed x10, local copies, waits for them, and re-layouts  2.98 us
  transfers between devices with their start and end apart: 16, of which 7 were waited for; matrix products, arithmetic and copies ran while one was open for 3% of the time, Pallas kernels for 21%

commit v1 on v0

--- a/solution.py
+++ b/solution.py
@@ -1,3 +1,4 @@
+import itertools
 import math
 
 import jax
@@ -13,9 +14,10 @@
 LANES = 128
 TURN = 16
 LEAD = 16
-PAIR = 2
+PAIR = 4
 UNROLL = 4
 PITCH = 36
+ORDER = (5, 1, 4, 7, 2, 3, 6)
 POWER = 12
 FLOOR = 2.0**-10.25
 REACH = 2.0**10.25
@@ -70,26 +72,25 @@
 def filter_kernel(frames, taps, grid, largest, window):
     depth = taps.shape[0]
     count = frames.shape[1]
-    window[pl.ds(0, LEAD), :] = jnp.zeros((LEAD, LANES), jnp.float32)
-
-    def step(number, most):
-        part = number // SLOW
-        slow = number % SLOW
+    window[:, pl.ds(0, LEAD), :] = jnp.zeros((2, LEAD, LANES), jnp.float32)
+
+    def step(slow, most):
         columns = pl.ds(pl.multiple_of(slow * LANES, LANES), LANES)
-        window[pl.ds(LEAD, count), :] = frames[part, :, columns].astype(jnp.float32)
         weights = [taps[pl.ds(k, 1), columns] for k in range(depth)]
-        for block in range(count // 8):
+        for part in range(2):
+            window[part, pl.ds(LEAD, count), :] = frames[part, :, columns].astype(jnp.float32)
+        for part, block in itertools.product(range(2), range(count // 8)):
             total = None
             for k in range(depth):
                 if 8 * block + 7 < k:
                     continue
-                term = weights[k] * window[pl.ds(LEAD + block * 8 - k, 8), :]
+                term = weights[k] * window[part, pl.ds(LEAD + block * 8 - k, 8), :]
                 total = term if total is None else total + term
             grid[part, slow, pl.ds(block * 8, 8), :] = total
             most = jnp.maximum(most, jnp.abs(total))
         return most
 
-    largest[...] = lax.fori_loop(0, 2 * SLOW, step, jnp.zeros((8, LANES), jnp.float32))
+    largest[...] = lax.fori_loop(0, SLOW, step, jnp.zeros((8, LANES), jnp.float32), unroll=2)
 
 
 def filtered(frames, taps):
@@ -103,18 +104,18 @@
         ],
         in_specs=[whole] * 2,
         out_specs=[whole] * 2,
-        scratch_shapes=[pltpu.VMEM((LEAD + count, LANES), jnp.float32)],
+        scratch_shapes=[pltpu.VMEM((2, LEAD + count, LANES), jnp.float32)],
         compiler_params=pltpu.CompilerParams(vmem_limit_bytes=12 * 1024 * 1024),
         name="filter",
     )(frames, taps)
 
 
-def encode_kernel(place, edge, taps, grid, largest, twist, matrix, *rest):
+def encode_kernel(edge, taps, grid, largest, twist, matrix, *rest):
     pieces = rest[:8]
     window, head, half, split_high, split_low, rows = rest[8:]
     depth = taps.shape[0]
     count = grid.shape[2]
-    me = place[0]
+    me = lax.axis_index("tm")
     window[pl.ds(LEAD, LEAD), :] = jnp.zeros((LEAD, LANES), jnp.float32)
 
     def head_step(number, most):
@@ -197,7 +198,7 @@
         pieces[d][pl.ds(2 * share * SLOW, 16), :] = jnp.concatenate([scale, scale], axis=0).astype(jnp.bfloat16)
 
 
-def encode(place, edge, taps, grid, largest, twist, matrix):
+def encode(edge, taps, grid, largest, twist, matrix):
     count = grid.shape[2]
     channels = taps.shape[1]
     piece = jax.ShapeDtypeStruct((2 * channels // 8 + 16, count), jnp.bfloat16)
@@ -205,7 +206,7 @@
     return pl.pallas_call(
         encode_kernel,
         out_shape=[piece] * 8,
-        in_specs=[pl.BlockSpec(memory_space=pltpu.SMEM)] + [whole] * 6,
+        in_specs=[whole] * 6,
         out_specs=[whole] * 8,
         scratch_shapes=[
             pltpu.VMEM((2 * LEAD, LANES), jnp.float32),
@@ -217,15 +218,15 @@
         ],
         compiler_params=pltpu.CompilerParams(vmem_limit_bytes=20 * 1024 * 1024),
         name="encode",
-    )(place, edge, taps, grid, largest, twist, matrix)
-
-
-def decode_kernel(place, *rest):
+    )(edge, taps, grid, largest, twist, matrix)
+
+
+def decode_kernel(*rest):
     pieces = rest[:8]
     output = rest[-1]
     width = output.shape[2]
     half = (pieces[0].shape[0] - 16) // 2
-    me = place[0]
+    me = lax.axis_index("tm")
     base = pl.program_id(0) * width
     inverse = [1.0 / pieces[d][pl.ds(2 * half, 16), :].astype(jnp.float32) for d in range(8)]
 
@@ -251,18 +252,18 @@
     lax.fori_loop(0, width // 16, step, 0, unroll=4)
 
 
-def decode(place, pieces, stream, streams, before):
+def decode(pieces, stream, streams, before):
     half = (pieces[0].shape[0] - 16) // 2
     blocks = 4
     shape = (streams, 2, half, 8 * LANES)
     whole = pl.BlockSpec(memory_space=pltpu.VMEM)
-    operands = [place, *pieces]
-    in_specs = [pl.BlockSpec(memory_space=pltpu.SMEM)] + [whole] * 8
+    operands = [*pieces]
+    in_specs = [whole] * 8
     aliases = {}
     if before is not None:
         operands.append(before)
         in_specs.append(pl.BlockSpec(memory_space=pl.ANY))
-        aliases = {9: 0}
+        aliases = {8: 0}
     return pl.pallas_call(
         decode_kernel,
         grid=(blocks,),
@@ -280,25 +281,29 @@
     channels = taps.shape[1]
     count = signal.shape[2] // channels
     size = lax.axis_size("tm")
-    place = lax.axis_index("tm").astype(jnp.int32)[None]
     twist, matrix = tables(channels)
     route = [(i, i + 1) for i in range(size - 1)]
-    tail = signal[:, :, (count - LEAD) * channels :]
-    edges = [lax.ppermute(tail[stream], "tm", route) for stream in range(streams)]
+    last = (count - LEAD) * channels
+    tail = signal[:1, :, last:]
+    edge = lax.ppermute(tail, "tm", route)
+    held, tail = lax.optimization_barrier((signal, tail))
     arrived = []
-    held = signal
     for stream in range(streams):
         frames = held[stream].reshape(2, count, channels)
         grid, largest = filtered(frames, taps)
-        edge = edges[stream].reshape(2, LEAD, channels)
-        pieces = list(encode(place, edge, taps, grid, largest, twist, matrix))
+        near = edge.reshape(2, LEAD, channels)
+        if stream + 1 < streams:
+            tail = held[stream + 1 : stream + 2, :, last:]
+            tail, largest = lax.optimization_barrier((tail, largest))
+            edge = lax.ppermute(tail, "tm", route)
+        pieces = list(encode(near, taps, grid, largest, twist, matrix))
         held, pieces[0] = lax.optimization_barrier((held, pieces[0]))
-        for d in range(1, size):
+        for d in ORDER:
             pieces[d] = lax.ppermute(pieces[d], "tm", [(i, i ^ d) for i in range(size)])
         arrived.append(pieces)
     output = None
     for stream in range(streams):
-        output = decode(place, arrived[stream], stream, streams, output)
+        output = decode(arrived[stream], stream, streams, output)
     return output
 
 

time: 105 us -> 104 us (level)
  Pallas kernels: 31.8 us -> 29.7 us
  waiting for transfers between devices: 29.1 us -> 30.9 us
  starting transfers between devices: 38.7 us -> 37.5 us
    slice x0 -> x2, local copies, waits for them, and re-layouts: none -> 2.41 us  [the longest x1 1.28 us: shards(): tail = signal[:1, :, last:]]
    squeeze x1 -> x0, local copies, waits for them, and re-layouts: 2.24 us -> none  [shards(): tail[stream]]
    ppermute x14, waiting for transfers between devices: 20.1 us -> 21.9 us  [shards(): pieces[d] = lax.ppermute(pieces[d], 'tm', [(i, i ^ d) for i in range(size)])]
    ppermute x14, starting transfers between devices: 32.6 us -> 31.1 us  [shards(): pieces[d] = lax.ppermute(pieces[d], 'tm', [(i, i ^ d) for i in range(size)])]
    pallas_call x2, Pallas kernels: 11.5 us -> 10.5 us  [filtered(): pl.pallas_call(filter_kernel, out_shape=[jax.ShapeDtypeStruct((2, SLOW, c...]
  transfers between devices with their start and end apart: 16 -> 16, of which waited for: 7 -> 7; matrix products, arithmetic and copies ran while one was open for 3% -> 4% of each run, Pallas kernels for 21% -> 19%
where the time goes in v1:
time: 104 us
  starting transfers between devices  37.5 us (36%)
  waiting for transfers between devices  30.9 us (30%)
  Pallas kernels  29.7 us (29%)
  local copies, waits for them, and re-layouts  5.41 us (5%)
    ppermute x14, starting transfers between devices, shards(): pieces[d] = lax.ppermute(pieces[d], 'tm', [(i, i ^ d) for i in range(size)])  31.1 us
    ppermute x14, waiting for transfers between devices, shards(): pieces[d] = lax.ppermute(pieces[d], 'tm', [(i, i ^ d) for i in range(size)])  21.9 us
    pallas_call x2, Pallas kernels, encode(): pl.pallas_call(encode_kernel, out_shape=[piece] * 8, in_specs=[whole] * 6...  12 us
    pallas_call x2, Pallas kernels, filtered(): pl.pallas_call(filter_kernel, out_shape=[jax.ShapeDtypeStruct((2, SLOW, c...  10.5 us
    ppermute x2, waiting for transfers between devices, shards(): edge = lax.ppermute(tail, 'tm', route)  8.96 us
    pallas_call x2, Pallas kernels, decode(): pl.pallas_call(decode_kernel, grid=(blocks,), out_shape=jax.ShapeDtypeStr...  7.25 us
    ppermute x2, starting transfers between devices, shards(): edge = lax.ppermute(tail, 'tm', route)  6.48 us
    unnamed x10, local copies, waits for them, and re-layouts  2.98 us
  transfers between devices with their start and end apart: 16, of which 7 were waited for; matrix products, arithmetic and copies ran while one was open for 4% of the time, Pallas kernels for 19%

profile of v1, /device:TPU:192, one launch (start us, length us, event | category | flops | bytes accessed | tf_op | source)
XLA Modules:
  0.0 103.7 jit_solution(6182860180838857610)
XLA Ops:
  0.0 1.3 %slice.12 = bf16[1,2,65536]{2,1,0:T(2,128)(2,1)S(1)} slice(bf16[2,2,524288]{2,1,0:T(2,128)(2,1)} %param.4), slice={[0:1], [0:2], [458752:524288]} | slice | bytes 524288 | tf_op jit(solution)/shard_map/slice | solution.py:287
  1.3 3.5 %collective-permute-start = (bf16[1,2,65536]{2,1,0:T(2,128)(2,1)S(1)}, bf16[1,2,65536]{2,1,0:T(2,128)(2,1)S(1)}, u32[]{:S(2)}, u32[]{:S(2)}) collective-permute-start(bf16[1,2,65536]{2,1,0:T(2,128)(2,1)S(1)} %slice.12), channel_id=1, source_target_pairs={{0,1},{1,2},{2,3},{3,4},{4,5},{5,6},{6,7},{8,9},{9,10},{10,11},{11... | collective-permute-start | bytes 786440 | tf_op jit(solution)/shard_map/ppermute | solution.py:288
  4.8 1.1 %slice.14 = bf16[1,2,65536]{2,1,0:T(2,128)(2,1)S(1)} slice(bf16[2,2,524288]{2,1,0:T(2,128)(2,1)} %param.4), slice={[1:2], [0:2], [458752:524288]} | slice | bytes 524288 | tf_op jit(solution)/shard_map/slice | solution.py:296
  5.9 0.0 copy-start
  5.9 0.0 copy-start.1
  6.0 0.0 copy-start.2
  6.0 1.3 %copy.15 = bf16[1,2,128,4096]{3,2,1,0:T(8,128)(2,1)S(1)} copy(bf16[1,2,128,4096]{3,1,2,0:T(2,128)(2,1)S(1)} %bitcast.24) | data formatting | bytes 4194304
  7.3 5.2 %filter.2 = (f32[2,32,128,128]{3,2,1,0:T(8,128)S(1)}, f32[8,128]{1,0:T(8,128)S(1)}) custom-call(bf16[2,128,4096]{2,1,0:T(8,128)(2,1)S(1)} %bitcast.20, f32[16,4096]{1,0:T(8,128)S(1)} %copy-done), custom_call_target="tpu_custom_call" | custom-call | tf_op jit(solution)/shard_map/filter/pallas_call | solution.py:99
  12.6 0.0 collective-permute-done
  12.6 0.2 copy.17
  12.8 0.0 slice-start.1
  12.8 6.0 %encode.2 = (bf16[1040,128]{1,0:T(8,128)(2,1)S(1)}, bf16[1040,128]{1,0:T(8,128)(2,1)S(1)}, bf16[1040,128]{1,0:T(8,128)(2,1)S(1)}, bf16[1040,128]{1,0:T(8,128)(2,...) custom-call(bf16[2,16,4096]{2,1,0:T(8,128)(2,1)S(1)} %bitcast.23, ...), custom_call_target="tpu_custom_call" | custom-call | tf_op jit(solution)/shard_map/encode/pallas_call | solution.py:206
  18.8 1.4 %collective-permute-start.9 = (bf16[1040,128]{1,0:T(8,128)(2,1)S(1)}, bf16[1040,128]{1,0:T(8,128)(2,1)S(1)}, u32[]{:S(2)}, u32[]{:S(2)}) collective-permute-start(bf16[1040,128]{1,0:T(8,128)(2,1)S(1)} %get-tuple-element.50), channel_id=1, source_target_pairs={{0,1},{1,0},{2,3},{3,2},{4,5},{5,4},{6,7},{7,6},{8,9},{9,8},{10,11... | collective-permute-start | bytes 798728 | tf_op jit(solution)/shard_map/ppermute | solution.py:302
  20.2 1.5 %collective-permute-start.10 = (bf16[1040,128]{1,0:T(8,128)(2,1)S(1)}, bf16[1040,128]{1,0:T(8,128)(2,1)S(1)}, u32[]{:S(2)}, u32[]{:S(2)}) collective-permute-start(bf16[1040,128]{1,0:T(8,128)(2,1)S(1)} %get-tuple-element.51), channel_id=1, source_target_pairs={{0,2},{1,3},{2,0},{3,1},{4,6},{5,7},{6,4},{7,5},{8,10},{9,11},{10,... | collective-permute-start | bytes 798728 | tf_op jit(solution)/shard_map/ppermute | solution.py:302
  21.7 0.6 collective-permute-start.11
  22.3 3.0 %collective-permute-start.12 = (bf16[1040,128]{1,0:T(8,128)(2,1)S(1)}, bf16[1040,128]{1,0:T(8,128)(2,1)S(1)}, u32[]{:S(2)}, u32[]{:S(2)}) collective-permute-start(bf16[1040,128]{1,0:T(8,128)(2,1)S(1)} %get-tuple-element.53), channel_id=1, source_target_pairs={{0,4},{1,5},{2,6},{3,7},{4,0},{5,1},{6,2},{7,3},{8,12},{9,13},{10,... | collective-permute-start | bytes 798728 | tf_op jit(solution)/shard_map/ppermute | solution.py:302
  25.3 3.0 %collective-permute-start.1 = (bf16[1,2,65536]{2,1,0:T(2,128)(2,1)S(1)}, bf16[1,2,65536]{2,1,0:T(2,128)(2,1)S(1)}, u32[]{:S(2)}, u32[]{:S(2)}) collective-permute-start(bf16[1,2,65536]{2,1,0:T(2,128)(2,1)S(1)} %slice.14), channel_id=1, source_target_pairs={{0,1},{1,2},{2,3},{3,4},{4,5},{5,6},{6,7},{8,9},{9,10},{10,11},{11... | collective-permute-start | bytes 786440 | tf_op jit(solution)/shard_map/ppermute | solution.py:298
  28.3 9.0 %collective-permute-done.1 = bf16[1,2,65536]{2,1,0:T(2,128)(2,1)S(1)} collective-permute-done((bf16[1,2,65536]{2,1,0:T(2,128)(2,1)S(1)}, bf16[1,2,65536]{2,1,0:T(2,128)(2,1)S(1)}, u32[]{:S(2)}, u32[]{:S(2)}) %collective-permute-start.1) | collective-permute-done | bytes 262176 | tf_op jit(solution)/shard_map/ppermute | solution.py:298
  37.3 0.1 copy.16
  37.5 10.4 %collective-permute-start.13 = (bf16[1040,128]{1,0:T(8,128)(2,1)S(1)}, bf16[1040,128]{1,0:T(8,128)(2,1)S(1)}, u32[]{:S(2)}, u32[]{:S(2)}) collective-permute-start(bf16[1040,128]{1,0:T(8,128)(2,1)S(1)} %get-tuple-element.54), channel_id=1, source_target_pairs={{0,5},{1,4},{2,7},{3,6},{4,1},{5,0},{6,3},{7,2},{8,13},{9,12},{10,... | collective-permute-start | bytes 798728 | tf_op jit(solution)/shard_map/ppermute | solution.py:302
  47.8 1.3 %copy.14 = bf16[1,2,128,4096]{3,2,1,0:T(8,128)(2,1)S(1)} copy(bf16[1,2,128,4096]{3,1,2,0:T(2,128)(2,1)S(1)} %bitcast.25) | data formatting | bytes 4194304
  49.2 5.2 %filter.3 = (f32[2,32,128,128]{3,2,1,0:T(8,128)S(1)}, f32[8,128]{1,0:T(8,128)S(1)}) custom-call(bf16[2,128,4096]{2,1,0:T(8,128)(2,1)S(1)} %bitcast.21, f32[16,4096]{1,0:T(8,128)S(1)} %copy-done), custom_call_target="tpu_custom_call" | custom-call | tf_op jit(solution)/shard_map/filter/pallas_call | solution.py:99
  54.4 6.0 %encode.3 = (bf16[1040,128]{1,0:T(8,128)(2,1)S(1)}, bf16[1040,128]{1,0:T(8,128)(2,1)S(1)}, bf16[1040,128]{1,0:T(8,128)(2,1)S(1)}, bf16[1040,128]{1,0:T(8,128)(2,...) custom-call(bf16[2,16,4096]{2,1,0:T(8,128)(2,1)S(1)} %bitcast.22, ...), custom_call_target="tpu_custom_call" | custom-call | tf_op jit(solution)/shard_map/encode/pallas_call | solution.py:206
  60.4 0.0 collective-permute-done.9.rest_1_
  60.4 1.1 %collective-permute-start.14 = (bf16[1040,128]{1,0:T(8,128)(2,1)S(1)}, bf16[1040,128]{1,0:T(8,128)(2,1)S(1)}, u32[]{:S(2)}, u32[]{:S(2)}) collective-permute-start(bf16[1040,128]{1,0:T(8,128)(2,1)S(1)} %get-tuple-element.55), channel_id=1, source_target_pairs={{0,6},{1,7},{2,4},{3,5},{4,2},{5,3},{6,0},{7,1},{8,14},{9,15},{10,... | collective-permute-start | bytes 798728 | tf_op jit(solution)/shard_map/ppermute | solution.py:302
  61.5 0.0 collective-permute-done.10.rest_2_
  61.5 2.6 %collective-permute-start.15 = (bf16[1040,128]{1,0:T(8,128)(2,1)S(1)}, bf16[1040,128]{1,0:T(8,128)(2,1)S(1)}, u32[]{:S(2)}, u32[]{:S(2)}) collective-permute-start(bf16[1040,128]{1,0:T(8,128)(2,1)S(1)} %get-tuple-element.56), channel_id=1, source_target_pairs={{0,7},{1,6},{2,5},{3,4},{4,3},{5,2},{6,1},{7,0},{8,15},{9,14},{10,... | collective-permute-start | bytes 798728 | tf_op jit(solution)/shard_map/ppermute | solution.py:302
  64.1 0.0 collective-permute-done.11.rest_3_
  64.1 1.1 %collective-permute-start.2 = (bf16[1040,128]{1,0:T(8,128)(2,1)S(1)}, bf16[1040,128]{1,0:T(8,128)(2,1)S(1)}, u32[]{:S(2)}, u32[]{:S(2)}) collective-permute-start(bf16[1040,128]{1,0:T(8,128)(2,1)S(1)} %get-tuple-element.42), channel_id=1, source_target_pairs={{0,1},{1,0},{2,3},{3,2},{4,5},{5,4},{6,7},{7,6},{8,9},{9,8},{10,11... | collective-permute-start | bytes 798728 | tf_op jit(solution)/shard_map/ppermute | solution.py:302
  65.2 0.0 collective-permute-done.12.rest_4_
  65.2 0.2 collective-permute-start.3
  65.4 0.0 collective-permute-done.13.rest_5_
  65.4 2.2 %collective-permute-start.4 = (bf16[1040,128]{1,0:T(8,128)(2,1)S(1)}, bf16[1040,128]{1,0:T(8,128)(2,1)S(1)}, u32[]{:S(2)}, u32[]{:S(2)}) collective-permute-start(bf16[1040,128]{1,0:T(8,128)(2,1)S(1)} %get-tuple-element.44), channel_id=1, source_target_pairs={{0,3},{1,2},{2,1},{3,0},{4,7},{5,6},{6,5},{7,4},{8,11},{9,10},{10,... | collective-permute-start | bytes 798728 | tf_op jit(solution)/shard_map/ppermute | solution.py:302
  67.6 2.7 %collective-permute-done.14.rest_6_ = bf16[1040,128]{1,0:T(8,128)(2,1)S(1)} collective-permute-done((bf16[1040,128]{1,0:T(8,128)(2,1)S(1)}, bf16[1040,128]{1,0:T(8,128)(2,1)S(1)}, u32[]{:S(2)}, u32[]{:S(2)}) %collective-permute-start.14) | collective-permute-done | bytes 266272 | tf_op jit(solution)/shard_map/ppermute | solution.py:302
  70.3 0.3 collective-permute-start.5
  70.5 3.9 %collective-permute-done.15.rest_7_ = bf16[1040,128]{1,0:T(8,128)(2,1)S(1)} collective-permute-done((bf16[1040,128]{1,0:T(8,128)(2,1)S(1)}, bf16[1040,128]{1,0:T(8,128)(2,1)S(1)}, u32[]{:S(2)}, u32[]{:S(2)}) %collective-permute-start.15) | collective-permute-done | bytes 266272 | tf_op jit(solution)/shard_map/ppermute | solution.py:302
  74.5 2.1 %collective-permute-start.6 = (bf16[1040,128]{1,0:T(8,128)(2,1)S(1)}, bf16[1040,128]{1,0:T(8,128)(2,1)S(1)}, u32[]{:S(2)}, u32[]{:S(2)}) collective-permute-start(bf16[1040,128]{1,0:T(8,128)(2,1)S(1)} %get-tuple-element.46), channel_id=1, source_target_pairs={{0,5},{1,4},{2,7},{3,6},{4,1},{5,0},{6,3},{7,2},{8,13},{9,12},{10,... | collective-permute-start | bytes 798728 | tf_op jit(solution)/shard_map/ppermute | solution.py:302
  76.5 5.1 %collective-permute-done.2.rest_1_ = bf16[1040,128]{1,0:T(8,128)(2,1)S(1)} collective-permute-done((bf16[1040,128]{1,0:T(8,128)(2,1)S(1)}, bf16[1040,128]{1,0:T(8,128)(2,1)S(1)}, u32[]{:S(2)}, u32[]{:S(2)}) %collective-permute-start.2) | collective-permute-done | bytes 266272 | tf_op jit(solution)/shard_map/ppermute | solution.py:302
  81.6 4.6 %collective-permute-start.7 = (bf16[1040,128]{1,0:T(8,128)(2,1)S(1)}, bf16[1040,128]{1,0:T(8,128)(2,1)S(1)}, u32[]{:S(2)}, u32[]{:S(2)}) collective-permute-start(bf16[1040,128]{1,0:T(8,128)(2,1)S(1)} %get-tuple-element.47), channel_id=1, source_target_pairs={{0,6},{1,7},{2,4},{3,5},{4,2},{5,3},{6,0},{7,1},{8,14},{9,15},{10,... | collective-permute-start | bytes 798728 | tf_op jit(solution)/shard_map/ppermute | solution.py:302
  86.2 0.0 collective-permute-done.3.rest_2_
  86.2 0.0 collective-permute-start.8
  86.2 3.6 %decode.2.rest_8_ = f32[2,2,512,1024]{3,2,1,0:T(8,128)} custom-call(bf16[1040,128]{1,0:T(8,128)(2,1)S(1)} %get-tuple-element.49.rest_0_, bf16[1040,128]{1,0:T(8,128)(2,1)S(1)} %collective-permute-done.9.rest_1_, bf16[1040,128]{1,0:T(8,128)(2,1)S(1)} %collective-permute-done.10.rest_2_, bf16[1040,128]{1,0:T(8,128)(2,1)S(1)} %collective-permute-done.11.rest_3_, ...), custom_call_target="tpu_custom_call" | custom-call | tf_op jit(solution)/shard_map/decode/pallas_call | solution.py:267
  89.8 0.0 collective-permute-done.4.rest_3_
  89.8 0.0 collective-permute-done.5.rest_4_
  89.8 0.3 collective-permute-done.6.rest_5_
  90.1 4.5 %collective-permute-done.7.rest_6_ = bf16[1040,128]{1,0:T(8,128)(2,1)S(1)} collective-permute-done((bf16[1040,128]{1,0:T(8,128)(2,1)S(1)}, bf16[1040,128]{1,0:T(8,128)(2,1)S(1)}, u32[]{:S(2)}, u32[]{:S(2)}) %collective-permute-start.7) | collective-permute-done | bytes 266272 | tf_op jit(solution)/shard_map/ppermute | solution.py:302
  94.6 5.5 %collective-permute-done.8.rest_7_ = bf16[1040,128]{1,0:T(8,128)(2,1)S(1)} collective-permute-done((bf16[1040,128]{1,0:T(8,128)(2,1)S(1)}, bf16[1040,128]{1,0:T(8,128)(2,1)S(1)}, u32[]{:S(2)}, u32[]{:S(2)}) %collective-permute-start.8) | collective-permute-done | bytes 266272 | tf_op jit(solution)/shard_map/ppermute | solution.py:302
  100.1 3.6 %decode.3 = f32[2,2,512,1024]{3,2,1,0:T(8,128)} custom-call(bf16[1040,128]{1,0:T(8,128)(2,1)S(1)} %get-tuple-element.41.rest_0_, bf16[1040,128]{1,0:T(8,128)(2,1)S(1)} %collective-permute-done.2.rest_1_, bf16[1040,128]{1,0:T(8,128)(2,1)S(1)} %collective-permute-done.3.rest_2_, ...), custom_call_target="tpu_custom_call", output_to_operand_aliasing={{}: (8, {})} | custom-call | tf_op jit(solution)/shard_map/decode/pallas_call | solution.py:267
  (6 shorter events, 0.0 us)
Async XLA Ops:
  0.0 6.0 %slice-start = ((bf16[2,2,524288]{2,1,0:T(2,128)(2,1)}), bf16[1,2,524288]{2,1,0:T(2,128)(2,1)S(1)}, s32[]{:S(2)}) async-start(bf16[2,2,524288]{2,1,0:T(2,128)(2,1)} %param.4), calls=%async_computation | async-start | bytes 4194304 | tf_op jit(solution)/shard_map/slice | solution.py:292
  1.3 11.3 %collective-permute-start = (bf16[1,2,65536]{2,1,0:T(2,128)(2,1)S(1)}, bf16[1,2,65536]{2,1,0:T(2,128)(2,1)S(1)}, u32[]{:S(2)}, u32[]{:S(2)}) collective-permute-start(bf16[1,2,65536]{2,1,0:T(2,128)(2,1)S(1)} %slice.12), channel_id=1, source_target_pairs={{0,1},{1,2},{2,3},{3,4},{4,5},{5,6},{6,7},{8,9},{9,10},{10,11},{11... | collective-permute-start | bytes 786440 | tf_op jit(solution)/shard_map/ppermute | solution.py:288
  5.9 1.4 %copy-start = (f32[16,4096]{1,0:T(8,128)S(1)}, f32[16,4096]{1,0:T(8,128)}, u32[]{:S(2)}) copy-start(f32[16,4096]{1,0:T(8,128)} %taps.7) | copy-start | bytes 786436
  5.9 6.8 %copy-start.1 = (bf16[256,768]{1,0:T(8,128)(2,1)S(1)}, bf16[256,768]{1,0:T(8,128)(2,1)}, u32[]{:S(2)}) copy-start(bf16[256,768]{1,0:T(8,128)(2,1)} %constant.5.clone.matrix) | copy-start | bytes 1179652
  6.0 6.8 %copy-start.2 = (f32[2,32,128]{2,1,0:T(8,128)S(1)}, f32[2,32,128]{2,1,0:T(8,128)}, u32[]{:S(2)}) copy-start(f32[2,32,128]{2,1,0:T(8,128)} %constant.4.clone.twist) | copy-start | bytes 98308
  12.8 35.1 %slice-start.1 = ((bf16[2,2,524288]{2,1,0:T(2,128)(2,1)}), bf16[1,2,524288]{2,1,0:T(2,128)(2,1)S(1)}, s32[]{:S(2)}) async-start(bf16[2,2,524288]{2,1,0:T(2,128)(2,1)} %param.4), calls=%async_computation.1 | async-start | bytes 4194304 | tf_op jit(solution)/shard_map/slice | solution.py:292
  18.8 41.6 %collective-permute-start.9 = (bf16[1040,128]{1,0:T(8,128)(2,1)S(1)}, bf16[1040,128]{1,0:T(8,128)(2,1)S(1)}, u32[]{:S(2)}, u32[]{:S(2)}) collective-permute-start(bf16[1040,128]{1,0:T(8,128)(2,1)S(1)} %get-tuple-element.50), channel_id=1, source_target_pairs={{0,1},{1,0},{2,3},{3,2},{4,5},{5,4},{6,7},{7,6},{8,9},{9,8},{10,11... | collective-permute-start | bytes 798728 | tf_op jit(solution)/shard_map/ppermute | solution.py:302
  20.2 41.3 %collective-permute-start.10 = (bf16[1040,128]{1,0:T(8,128)(2,1)S(1)}, bf16[1040,128]{1,0:T(8,128)(2,1)S(1)}, u32[]{:S(2)}, u32[]{:S(2)}) collective-permute-start(bf16[1040,128]{1,0:T(8,128)(2,1)S(1)} %get-tuple-element.51), channel_id=1, source_target_pairs={{0,2},{1,3},{2,0},{3,1},{4,6},{5,7},{6,4},{7,5},{8,10},{9,11},{10,... | collective-permute-start | bytes 798728 | tf_op jit(solution)/shard_map/ppermute | solution.py:302
  21.7 42.4 %collective-permute-start.11 = (bf16[1040,128]{1,0:T(8,128)(2,1)S(1)}, bf16[1040,128]{1,0:T(8,128)(2,1)S(1)}, u32[]{:S(2)}, u32[]{:S(2)}) collective-permute-start(bf16[1040,128]{1,0:T(8,128)(2,1)S(1)} %get-tuple-element.52), channel_id=1, source_target_pairs={{0,3},{1,2},{2,1},{3,0},{4,7},{5,6},{6,5},{7,4},{8,11},{9,10},{10,... | collective-permute-start | bytes 798728 | tf_op jit(solution)/shard_map/ppermute | solution.py:302
  22.3 42.9 %collective-permute-start.12 = (bf16[1040,128]{1,0:T(8,128)(2,1)S(1)}, bf16[1040,128]{1,0:T(8,128)(2,1)S(1)}, u32[]{:S(2)}, u32[]{:S(2)}) collective-permute-start(bf16[1040,128]{1,0:T(8,128)(2,1)S(1)} %get-tuple-element.53), channel_id=1, source_target_pairs={{0,4},{1,5},{2,6},{3,7},{4,0},{5,1},{6,2},{7,3},{8,12},{9,13},{10,... | collective-permute-start | bytes 798728 | tf_op jit(solution)/shard_map/ppermute | solution.py:302
  25.3 11.9 %collective-permute-start.1 = (bf16[1,2,65536]{2,1,0:T(2,128)(2,1)S(1)}, bf16[1,2,65536]{2,1,0:T(2,128)(2,1)S(1)}, u32[]{:S(2)}, u32[]{:S(2)}) collective-permute-start(bf16[1,2,65536]{2,1,0:T(2,128)(2,1)S(1)} %slice.14), channel_id=1, source_target_pairs={{0,1},{1,2},{2,3},{3,4},{4,5},{5,6},{6,7},{8,9},{9,10},{10,11},{11... | collective-permute-start | bytes 786440 | tf_op jit(solution)/shard_map/ppermute | solution.py:298
  37.5 27.9 %collective-permute-start.13 = (bf16[1040,128]{1,0:T(8,128)(2,1)S(1)}, bf16[1040,128]{1,0:T(8,128)(2,1)S(1)}, u32[]{:S(2)}, u32[]{:S(2)}) collective-permute-start(bf16[1040,128]{1,0:T(8,128)(2,1)S(1)} %get-tuple-element.54), channel_id=1, source_target_pairs={{0,5},{1,4},{2,7},{3,6},{4,1},{5,0},{6,3},{7,2},{8,13},{9,12},{10,... | collective-permute-start | bytes 798728 | tf_op jit(solution)/shard_map/ppermute | solution.py:302
  60.4 9.9 %collective-permute-start.14 = (bf16[1040,128]{1,0:T(8,128)(2,1)S(1)}, bf16[1040,128]{1,0:T(8,128)(2,1)S(1)}, u32[]{:S(2)}, u32[]{:S(2)}) collective-permute-start(bf16[1040,128]{1,0:T(8,128)(2,1)S(1)} %get-tuple-element.55), channel_id=1, source_target_pairs={{0,6},{1,7},{2,4},{3,5},{4,2},{5,3},{6,0},{7,1},{8,14},{9,15},{10,... | collective-permute-start | bytes 798728 | tf_op jit(solution)/shard_map/ppermute | solution.py:302
  61.5 12.9 %collective-permute-start.15 = (bf16[1040,128]{1,0:T(8,128)(2,1)S(1)}, bf16[1040,128]{1,0:T(8,128)(2,1)S(1)}, u32[]{:S(2)}, u32[]{:S(2)}) collective-permute-start(bf16[1040,128]{1,0:T(8,128)(2,1)S(1)} %get-tuple-element.56), channel_id=1, source_target_pairs={{0,7},{1,6},{2,5},{3,4},{4,3},{5,2},{6,1},{7,0},{8,15},{9,14},{10,... | collective-permute-start | bytes 798728 | tf_op jit(solution)/shard_map/ppermute | solution.py:302
  64.1 17.5 %collective-permute-start.2 = (bf16[1040,128]{1,0:T(8,128)(2,1)S(1)}, bf16[1040,128]{1,0:T(8,128)(2,1)S(1)}, u32[]{:S(2)}, u32[]{:S(2)}) collective-permute-start(bf16[1040,128]{1,0:T(8,128)(2,1)S(1)} %get-tuple-element.42), channel_id=1, source_target_pairs={{0,1},{1,0},{2,3},{3,2},{4,5},{5,4},{6,7},{7,6},{8,9},{9,8},{10,11... | collective-permute-start | bytes 798728 | tf_op jit(solution)/shard_map/ppermute | solution.py:302
  65.2 21.0 %collective-permute-start.3 = (bf16[1040,128]{1,0:T(8,128)(2,1)S(1)}, bf16[1040,128]{1,0:T(8,128)(2,1)S(1)}, u32[]{:S(2)}, u32[]{:S(2)}) collective-permute-start(bf16[1040,128]{1,0:T(8,128)(2,1)S(1)} %get-tuple-element.43), channel_id=1, source_target_pairs={{0,2},{1,3},{2,0},{3,1},{4,6},{5,7},{6,4},{7,5},{8,10},{9,11},{10,... | collective-permute-start | bytes 798728 | tf_op jit(solution)/shard_map/ppermute | solution.py:302
  65.4 24.4 %collective-permute-start.4 = (bf16[1040,128]{1,0:T(8,128)(2,1)S(1)}, bf16[1040,128]{1,0:T(8,128)(2,1)S(1)}, u32[]{:S(2)}, u32[]{:S(2)}) collective-permute-start(bf16[1040,128]{1,0:T(8,128)(2,1)S(1)} %get-tuple-element.44), channel_id=1, source_target_pairs={{0,3},{1,2},{2,1},{3,0},{4,7},{5,6},{6,5},{7,4},{8,11},{9,10},{10,... | collective-permute-start | bytes 798728 | tf_op jit(solution)/shard_map/ppermute | solution.py:302
  70.3 19.5 %collective-permute-start.5 = (bf16[1040,128]{1,0:T(8,128)(2,1)S(1)}, bf16[1040,128]{1,0:T(8,128)(2,1)S(1)}, u32[]{:S(2)}, u32[]{:S(2)}) collective-permute-start(bf16[1040,128]{1,0:T(8,128)(2,1)S(1)} %get-tuple-element.45), channel_id=1, source_target_pairs={{0,4},{1,5},{2,6},{3,7},{4,0},{5,1},{6,2},{7,3},{8,12},{9,13},{10,... | collective-permute-start | bytes 798728 | tf_op jit(solution)/shard_map/ppermute | solution.py:302
  74.5 15.6 %collective-permute-start.6 = (bf16[1040,128]{1,0:T(8,128)(2,1)S(1)}, bf16[1040,128]{1,0:T(8,128)(2,1)S(1)}, u32[]{:S(2)}, u32[]{:S(2)}) collective-permute-start(bf16[1040,128]{1,0:T(8,128)(2,1)S(1)} %get-tuple-element.46), channel_id=1, source_target_pairs={{0,5},{1,4},{2,7},{3,6},{4,1},{5,0},{6,3},{7,2},{8,13},{9,12},{10,... | collective-permute-start | bytes 798728 | tf_op jit(solution)/shard_map/ppermute | solution.py:302
  81.6 13.0 %collective-permute-start.7 = (bf16[1040,128]{1,0:T(8,128)(2,1)S(1)}, bf16[1040,128]{1,0:T(8,128)(2,1)S(1)}, u32[]{:S(2)}, u32[]{:S(2)}) collective-permute-start(bf16[1040,128]{1,0:T(8,128)(2,1)S(1)} %get-tuple-element.47), channel_id=1, source_target_pairs={{0,6},{1,7},{2,4},{3,5},{4,2},{5,3},{6,0},{7,1},{8,14},{9,15},{10,... | collective-permute-start | bytes 798728 | tf_op jit(solution)/shard_map/ppermute | solution.py:302
  86.2 13.9 %collective-permute-start.8 = (bf16[1040,128]{1,0:T(8,128)(2,1)S(1)}, bf16[1040,128]{1,0:T(8,128)(2,1)S(1)}, u32[]{:S(2)}, u32[]{:S(2)}) collective-permute-start(bf16[1040,128]{1,0:T(8,128)(2,1)S(1)} %get-tuple-element.48), channel_id=1, source_target_pairs={{0,7},{1,6},{2,5},{3,4},{4,3},{5,2},{6,1},{7,0},{8,15},{9,14},{10,... | collective-permute-start | bytes 798728 | tf_op jit(solution)/shard_map/ppermute | solution.py:302

commit v2 on v1

--- a/solution.py
+++ b/solution.py
@@ -195,13 +195,13 @@
                 pieces[d][pl.ds((part * share + fast) * SLOW, SLOW), :] = rows[
                     part, pl.ds(start, SLOW), :
                 ].astype(jnp.bfloat16)
-        pieces[d][pl.ds(2 * share * SLOW, 16), :] = jnp.concatenate([scale, scale], axis=0).astype(jnp.bfloat16)
+        pieces[d][pl.ds(2 * share * SLOW, 8), :] = scale.astype(jnp.bfloat16)
 
 
 def encode(edge, taps, grid, largest, twist, matrix):
     count = grid.shape[2]
     channels = taps.shape[1]
-    piece = jax.ShapeDtypeStruct((2 * channels // 8 + 16, count), jnp.bfloat16)
+    piece = jax.ShapeDtypeStruct((2 * channels // 8 + 8, count), jnp.bfloat16)
     whole = pl.BlockSpec(memory_space=pltpu.VMEM)
     return pl.pallas_call(
         encode_kernel,
@@ -225,10 +225,10 @@
     pieces = rest[:8]
     output = rest[-1]
     width = output.shape[2]
-    half = (pieces[0].shape[0] - 16) // 2
+    half = (pieces[0].shape[0] - 8) // 2
     me = lax.axis_index("tm")
     base = pl.program_id(0) * width
-    inverse = [1.0 / pieces[d][pl.ds(2 * half, 16), :].astype(jnp.float32) for d in range(8)]
+    inverse = [1.0 / pieces[d][pl.ds(2 * half, 8), :].astype(jnp.float32) for d in range(8)]
 
     def step(number, carry):
         power = None
@@ -238,7 +238,7 @@
                 start = pl.multiple_of(part * half + base + number * 16, 16)
                 code = pieces[d][pl.ds(start, 16), :].astype(jnp.float32)
                 level = jnp.exp2(jnp.log2(jnp.abs(code)) * (1.0 / POWER)) - FLOOR
-                level = level * inverse[d]
+                level = level * inverse[d][:1]
                 found.append(jnp.where(code < 0.0, -level, level))
                 power = level * level if power is None else power + level * level
         total = jnp.sum(power, axis=1, keepdims=True)
@@ -249,11 +249,11 @@
                 output[0, part, pl.ds(pl.multiple_of(number * 16, 16), 16), lanes] = found[2 * d + part] * factor
         return carry
 
-    lax.fori_loop(0, width // 16, step, 0, unroll=4)
+    lax.fori_loop(0, width // 16, step, 0, unroll=8)
 
 
 def decode(pieces, stream, streams, before):
-    half = (pieces[0].shape[0] - 16) // 2
+    half = (pieces[0].shape[0] - 8) // 2
     blocks = 4
     shape = (streams, 2, half, 8 * LANES)
     whole = pl.BlockSpec(memory_space=pltpu.VMEM)
@@ -283,18 +283,16 @@
     size = lax.axis_size("tm")
     twist, matrix = tables(channels)
     route = [(i, i + 1) for i in range(size - 1)]
-    last = (count - LEAD) * channels
-    tail = signal[:1, :, last:]
-    edge = lax.ppermute(tail, "tm", route)
-    held, tail = lax.optimization_barrier((signal, tail))
+    tails = [signal[s : s + 1, :, (count - LEAD) * channels :] for s in range(streams)]
+    edge = lax.ppermute(tails[0], "tm", route)
     arrived = []
+    held = signal
     for stream in range(streams):
         frames = held[stream].reshape(2, count, channels)
         grid, largest = filtered(frames, taps)
         near = edge.reshape(2, LEAD, channels)
         if stream + 1 < streams:
-            tail = held[stream + 1 : stream + 2, :, last:]
-            tail, largest = lax.optimization_barrier((tail, largest))
+            tail, largest = lax.optimization_barrier((tails[stream + 1], largest))
             edge = lax.ppermute(tail, "tm", route)
         pieces = list(encode(near, taps, grid, largest, twist, matrix))
         held, pieces[0] = lax.optimization_barrier((held, pieces[0]))

time: 104 us -> 102 us (0.981)
  waiting for transfers between devices: 30.9 us -> 27.9 us
  starting transfers between devices: 37.5 us -> 39.5 us
    ppermute x2 -> x1, starting transfers between devices: 6.48 us -> 2.59 us  [shards(): edge = lax.ppermute(tail, 'tm', route)]
    ppermute x0 -> x1, starting transfers between devices: none -> 3.63 us  [shards(): edge = lax.ppermute(tails[0], 'tm', route)]
    ppermute x14, waiting for transfers between devices: 21.9 us -> 19.4 us  [shards(): pieces[d] = lax.ppermute(pieces[d], 'tm', [(i, i ^ d) for i in range(size)])]
    ppermute x14, starting transfers between devices: 31.1 us -> 33.3 us  [shards(): pieces[d] = lax.ppermute(pieces[d], 'tm', [(i, i ^ d) for i in range(size)])]
    slice x2 -> x1, local copies, waits for them, and re-layouts: 2.41 us -> 1.54 us  [shards(): signal[s:s + 1, :, (count - LEAD) * channels:]]
    ppermute x2 -> x1, waiting for transfers between devices: 8.96 us -> 8.56 us  [shards(): edge = lax.ppermute(tail, 'tm', route)]
  transfers between devices with their start and end apart: 16 -> 16, of which waited for: 7 -> 6; matrix products, arithmetic and copies ran while one was open for 4% -> 3% of each run, Pallas kernels for 19% -> 20%
where the time goes in v2:
time: 102 us; the launch traced here: 101 us
  starting transfers between devices  39.5 us (39%)
  Pallas kernels  29.4 us (29%)
  waiting for transfers between devices  27.9 us (27%)
  local copies, waits for them, and re-layouts  4.53 us (4%)
    ppermute x14, starting transfers between devices, shards(): pieces[d] = lax.ppermute(pieces[d], 'tm', [(i, i ^ d) for i in range(size)])  33.3 us
    ppermute x14, waiting for transfers between devices, shards(): pieces[d] = lax.ppermute(pieces[d], 'tm', [(i, i ^ d) for i in range(size)])  19.4 us
    pallas_call x2, Pallas kernels, encode(): pl.pallas_call(encode_kernel, out_shape=[piece] * 8, in_specs=[whole] * 6...  12 us
    pallas_call x2, Pallas kernels, filtered(): pl.pallas_call(filter_kernel, out_shape=[jax.ShapeDtypeStruct((2, SLOW, c...  10.5 us
    ppermute x1, waiting for transfers between devices, shards(): edge = lax.ppermute(tail, 'tm', route)  8.56 us
    pallas_call x2, Pallas kernels, decode(): pl.pallas_call(decode_kernel, grid=(blocks,), out_shape=jax.ShapeDtypeStr...  6.93 us
    ppermute x1, starting transfers between devices, shards(): edge = lax.ppermute(tails[0], 'tm', route)  3.63 us
    unnamed x10, local copies, waits for them, and re-layouts  2.98 us
  transfers between devices with their start and end apart: 16, of which 6 were waited for; matrix products, arithmetic and copies ran while one was open for 3% of the time, Pallas kernels for 20%

profile of v2, /device:TPU:192, one launch (start us, length us, event | category | flops | bytes accessed | tf_op | source)
XLA Modules:
  0.0 101.5 jit_solution(1144715187065125823)
XLA Ops:
  0.0 1.5 %fusion = (bf16[1,2,65536]{2,1,0:T(2,128)(2,1)S(1)}, bf16[1,2,65536]{2,1,0:T(2,128)(2,1)S(1)}) fusion(bf16[2,2,524288]{2,1,0:T(2,128)(2,1)} %param.4), kind=kLoop, calls=%fused_computation.4 | loop fusion | bytes 1048576 | tf_op jit(solution)/shard_map/slice | solution.py:286
  1.5 0.0 copy-start
  1.6 3.6 %collective-permute-start = (bf16[1,2,65536]{2,1,0:T(2,128)(2,1)S(1)}, bf16[1,2,65536]{2,1,0:T(2,128)(2,1)S(1)}, u32[]{:S(2)}, u32[]{:S(2)}) collective-permute-start(bf16[1,2,65536]{2,1,0:T(2,128)(2,1)S(1)} %get-tuple-element.56), channel_id=1, source_target_pairs={{0,1},{1,2},{2,3},{3,4},{4,5},{5,6},{6,7},{8,9},{9,10},{10,11},{11... | collective-permute-start | bytes 786440 | tf_op jit(solution)/shard_map/ppermute | solution.py:287
  5.2 0.0 copy-start.1
  5.2 0.0 copy-start.2
  5.2 1.3 %copy.15 = bf16[1,2,128,4096]{3,2,1,0:T(8,128)(2,1)S(1)} copy(bf16[1,2,128,4096]{3,1,2,0:T(2,128)(2,1)S(1)} %bitcast.24) | data formatting | bytes 4194304
  6.6 0.0 copy-done
  6.6 5.2 %filter.2 = (f32[2,32,128,128]{3,2,1,0:T(8,128)S(1)}, f32[8,128]{1,0:T(8,128)S(1)}) custom-call(bf16[2,128,4096]{2,1,0:T(8,128)(2,1)S(1)} %bitcast.20, f32[16,4096]{1,0:T(8,128)S(1)} %copy-done), custom_call_target="tpu_custom_call" | custom-call | tf_op jit(solution)/shard_map/filter/pallas_call | solution.py:99
  11.8 0.0 collective-permute-done
  11.8 0.2 copy.17
  12.0 0.0 slice-start.1
  12.0 6.0 %encode.2 = (bf16[1032,128]{1,0:T(8,128)(2,1)S(1)}, bf16[1032,128]{1,0:T(8,128)(2,1)S(1)}, bf16[1032,128]{1,0:T(8,128)(2,1)S(1)}, bf16[1032,128]{1,0:T(8,128)(2,...) custom-call(bf16[2,16,4096]{2,1,0:T(8,128)(2,1)S(1)} %bitcast.23, ...), custom_call_target="tpu_custom_call" | custom-call | tf_op jit(solution)/shard_map/encode/pallas_call | solution.py:206
  18.0 1.5 %collective-permute-start.9 = (bf16[1032,128]{1,0:T(8,128)(2,1)S(1)}, bf16[1032,128]{1,0:T(8,128)(2,1)S(1)}, u32[]{:S(2)}, u32[]{:S(2)}) collective-permute-start(bf16[1032,128]{1,0:T(8,128)(2,1)S(1)} %get-tuple-element.48), channel_id=1, source_target_pairs={{0,1},{1,0},{2,3},{3,2},{4,5},{5,4},{6,7},{7,6},{8,9},{9,8},{10,11... | collective-permute-start | bytes 792584 | tf_op jit(solution)/shard_map/ppermute | solution.py:300
  19.5 1.5 %collective-permute-start.10 = (bf16[1032,128]{1,0:T(8,128)(2,1)S(1)}, bf16[1032,128]{1,0:T(8,128)(2,1)S(1)}, u32[]{:S(2)}, u32[]{:S(2)}) collective-permute-start(bf16[1032,128]{1,0:T(8,128)(2,1)S(1)} %get-tuple-element.49), channel_id=1, source_target_pairs={{0,2},{1,3},{2,0},{3,1},{4,6},{5,7},{6,4},{7,5},{8,10},{9,11},{10,... | collective-permute-start | bytes 792584 | tf_op jit(solution)/shard_map/ppermute | solution.py:300
  21.0 0.8 collective-permute-start.11
  21.8 3.6 %collective-permute-start.12 = (bf16[1032,128]{1,0:T(8,128)(2,1)S(1)}, bf16[1032,128]{1,0:T(8,128)(2,1)S(1)}, u32[]{:S(2)}, u32[]{:S(2)}) collective-permute-start(bf16[1032,128]{1,0:T(8,128)(2,1)S(1)} %get-tuple-element.51), channel_id=1, source_target_pairs={{0,4},{1,5},{2,6},{3,7},{4,0},{5,1},{6,2},{7,3},{8,12},{9,13},{10,... | collective-permute-start | bytes 792584 | tf_op jit(solution)/shard_map/ppermute | solution.py:300
  25.3 2.6 %collective-permute-start.1 = (bf16[1,2,65536]{2,1,0:T(2,128)(2,1)S(1)}, bf16[1,2,65536]{2,1,0:T(2,128)(2,1)S(1)}, u32[]{:S(2)}, u32[]{:S(2)}) collective-permute-start(bf16[1,2,65536]{2,1,0:T(2,128)(2,1)S(1)} %get-tuple-element.35), channel_id=1, source_target_pairs={{0,1},{1,2},{2,3},{3,4},{4,5},{5,6},{6,7},{8,9},{9,10},{10,11},{11... | collective-permute-start | bytes 786440 | tf_op jit(solution)/shard_map/ppermute | solution.py:296
  27.9 8.6 %collective-permute-done.1 = bf16[1,2,65536]{2,1,0:T(2,128)(2,1)S(1)} collective-permute-done((bf16[1,2,65536]{2,1,0:T(2,128)(2,1)S(1)}, bf16[1,2,65536]{2,1,0:T(2,128)(2,1)S(1)}, u32[]{:S(2)}, u32[]{:S(2)}) %collective-permute-start.1) | collective-permute-done | bytes 262176 | tf_op jit(solution)/shard_map/ppermute | solution.py:296
  36.5 0.1 copy.16
  36.6 11.0 %collective-permute-start.13 = (bf16[1032,128]{1,0:T(8,128)(2,1)S(1)}, bf16[1032,128]{1,0:T(8,128)(2,1)S(1)}, u32[]{:S(2)}, u32[]{:S(2)}) collective-permute-start(bf16[1032,128]{1,0:T(8,128)(2,1)S(1)} %get-tuple-element.52), channel_id=1, source_target_pairs={{0,5},{1,4},{2,7},{3,6},{4,1},{5,0},{6,3},{7,2},{8,13},{9,12},{10,... | collective-permute-start | bytes 792584 | tf_op jit(solution)/shard_map/ppermute | solution.py:300
  47.7 1.3 %copy.14 = bf16[1,2,128,4096]{3,2,1,0:T(8,128)(2,1)S(1)} copy(bf16[1,2,128,4096]{3,1,2,0:T(2,128)(2,1)S(1)} %bitcast.25) | data formatting | bytes 4194304
  49.0 5.2 %filter.3 = (f32[2,32,128,128]{3,2,1,0:T(8,128)S(1)}, f32[8,128]{1,0:T(8,128)S(1)}) custom-call(bf16[2,128,4096]{2,1,0:T(8,128)(2,1)S(1)} %bitcast.21, f32[16,4096]{1,0:T(8,128)S(1)} %copy-done), custom_call_target="tpu_custom_call" | custom-call | tf_op jit(solution)/shard_map/filter/pallas_call | solution.py:99
  54.2 6.0 %encode.3 = (bf16[1032,128]{1,0:T(8,128)(2,1)S(1)}, bf16[1032,128]{1,0:T(8,128)(2,1)S(1)}, bf16[1032,128]{1,0:T(8,128)(2,1)S(1)}, bf16[1032,128]{1,0:T(8,128)(2,...) custom-call(bf16[2,16,4096]{2,1,0:T(8,128)(2,1)S(1)} %bitcast.22, ...), custom_call_target="tpu_custom_call" | custom-call | tf_op jit(solution)/shard_map/encode/pallas_call | solution.py:206
  60.2 0.0 collective-permute-done.9.rest_1_
  60.2 1.1 %collective-permute-start.14 = (bf16[1032,128]{1,0:T(8,128)(2,1)S(1)}, bf16[1032,128]{1,0:T(8,128)(2,1)S(1)}, u32[]{:S(2)}, u32[]{:S(2)}) collective-permute-start(bf16[1032,128]{1,0:T(8,128)(2,1)S(1)} %get-tuple-element.53), channel_id=1, source_target_pairs={{0,6},{1,7},{2,4},{3,5},{4,2},{5,3},{6,0},{7,1},{8,14},{9,15},{10,... | collective-permute-start | bytes 792584 | tf_op jit(solution)/shard_map/ppermute | solution.py:300
  61.4 0.0 collective-permute-done.10.rest_2_
  61.4 2.6 %collective-permute-start.15 = (bf16[1032,128]{1,0:T(8,128)(2,1)S(1)}, bf16[1032,128]{1,0:T(8,128)(2,1)S(1)}, u32[]{:S(2)}, u32[]{:S(2)}) collective-permute-start(bf16[1032,128]{1,0:T(8,128)(2,1)S(1)} %get-tuple-element.54), channel_id=1, source_target_pairs={{0,7},{1,6},{2,5},{3,4},{4,3},{5,2},{6,1},{7,0},{8,15},{9,14},{10,... | collective-permute-start | bytes 792584 | tf_op jit(solution)/shard_map/ppermute | solution.py:300
  63.9 0.0 collective-permute-done.11.rest_3_
  63.9 1.1 %collective-permute-start.2 = (bf16[1032,128]{1,0:T(8,128)(2,1)S(1)}, bf16[1032,128]{1,0:T(8,128)(2,1)S(1)}, u32[]{:S(2)}, u32[]{:S(2)}) collective-permute-start(bf16[1032,128]{1,0:T(8,128)(2,1)S(1)} %get-tuple-element.40), channel_id=1, source_target_pairs={{0,1},{1,0},{2,3},{3,2},{4,5},{5,4},{6,7},{7,6},{8,9},{9,8},{10,11... | collective-permute-start | bytes 792584 | tf_op jit(solution)/shard_map/ppermute | solution.py:300
  65.0 0.0 collective-permute-done.12.rest_4_
  65.0 0.2 collective-permute-start.3
  65.2 0.0 collective-permute-done.13.rest_5_
  65.2 2.2 %collective-permute-start.4 = (bf16[1032,128]{1,0:T(8,128)(2,1)S(1)}, bf16[1032,128]{1,0:T(8,128)(2,1)S(1)}, u32[]{:S(2)}, u32[]{:S(2)}) collective-permute-start(bf16[1032,128]{1,0:T(8,128)(2,1)S(1)} %get-tuple-element.42), channel_id=1, source_target_pairs={{0,3},{1,2},{2,1},{3,0},{4,7},{5,6},{6,5},{7,4},{8,11},{9,10},{10,... | collective-permute-start | bytes 792584 | tf_op jit(solution)/shard_map/ppermute | solution.py:300
  67.4 1.4 %collective-permute-done.14.rest_6_ = bf16[1032,128]{1,0:T(8,128)(2,1)S(1)} collective-permute-done((bf16[1032,128]{1,0:T(8,128)(2,1)S(1)}, bf16[1032,128]{1,0:T(8,128)(2,1)S(1)}, u32[]{:S(2)}, u32[]{:S(2)}) %collective-permute-start.14) | collective-permute-done | bytes 264224 | tf_op jit(solution)/shard_map/ppermute | solution.py:300
  68.9 1.0 %collective-permute-start.5 = (bf16[1032,128]{1,0:T(8,128)(2,1)S(1)}, bf16[1032,128]{1,0:T(8,128)(2,1)S(1)}, u32[]{:S(2)}, u32[]{:S(2)}) collective-permute-start(bf16[1032,128]{1,0:T(8,128)(2,1)S(1)} %get-tuple-element.43), channel_id=1, source_target_pairs={{0,4},{1,5},{2,6},{3,7},{4,0},{5,1},{6,2},{7,3},{8,12},{9,13},{10,... | collective-permute-start | bytes 792584 | tf_op jit(solution)/shard_map/ppermute | solution.py:300
  69.9 2.5 %collective-permute-done.15.rest_7_ = bf16[1032,128]{1,0:T(8,128)(2,1)S(1)} collective-permute-done((bf16[1032,128]{1,0:T(8,128)(2,1)S(1)}, bf16[1032,128]{1,0:T(8,128)(2,1)S(1)}, u32[]{:S(2)}, u32[]{:S(2)}) %collective-permute-start.15) | collective-permute-done | bytes 264224 | tf_op jit(solution)/shard_map/ppermute | solution.py:300
  72.4 2.4 %collective-permute-start.6 = (bf16[1032,128]{1,0:T(8,128)(2,1)S(1)}, bf16[1032,128]{1,0:T(8,128)(2,1)S(1)}, u32[]{:S(2)}, u32[]{:S(2)}) collective-permute-start(bf16[1032,128]{1,0:T(8,128)(2,1)S(1)} %get-tuple-element.44), channel_id=1, source_target_pairs={{0,5},{1,4},{2,7},{3,6},{4,1},{5,0},{6,3},{7,2},{8,13},{9,12},{10,... | collective-permute-start | bytes 792584 | tf_op jit(solution)/shard_map/ppermute | solution.py:300
  74.8 6.1 %collective-permute-done.2.rest_1_ = bf16[1032,128]{1,0:T(8,128)(2,1)S(1)} collective-permute-done((bf16[1032,128]{1,0:T(8,128)(2,1)S(1)}, bf16[1032,128]{1,0:T(8,128)(2,1)S(1)}, u32[]{:S(2)}, u32[]{:S(2)}) %collective-permute-start.2) | collective-permute-done | bytes 264224 | tf_op jit(solution)/shard_map/ppermute | solution.py:300
  80.9 3.8 %collective-permute-start.7 = (bf16[1032,128]{1,0:T(8,128)(2,1)S(1)}, bf16[1032,128]{1,0:T(8,128)(2,1)S(1)}, u32[]{:S(2)}, u32[]{:S(2)}) collective-permute-start(bf16[1032,128]{1,0:T(8,128)(2,1)S(1)} %get-tuple-element.45), channel_id=1, source_target_pairs={{0,6},{1,7},{2,4},{3,5},{4,2},{5,3},{6,0},{7,1},{8,14},{9,15},{10,... | collective-permute-start | bytes 792584 | tf_op jit(solution)/shard_map/ppermute | solution.py:300
  84.8 0.0 collective-permute-done.3.rest_2_
  84.8 0.4 collective-permute-start.8
  85.2 3.5 %decode.2.rest_8_ = f32[2,2,512,1024]{3,2,1,0:T(8,128)} custom-call(bf16[1032,128]{1,0:T(8,128)(2,1)S(1)} %get-tuple-element.47.rest_0_, bf16[1032,128]{1,0:T(8,128)(2,1)S(1)} %collective-permute-done.9.rest_1_, bf16[1032,128]{1,0:T(8,128)(2,1)S(1)} %collective-permute-done.10.rest_2_, bf16[1032,128]{1,0:T(8,128)(2,1)S(1)} %collective-permute-done.11.rest_3_, ...), custom_call_target="tpu_custom_call" | custom-call | tf_op jit(solution)/shard_map/decode/pallas_call | solution.py:267
  88.7 0.0 collective-permute-done.4.rest_3_
  88.7 0.0 collective-permute-done.5.rest_4_
  88.7 0.0 collective-permute-done.6.rest_5_
  88.7 4.2 %collective-permute-done.7.rest_6_ = bf16[1032,128]{1,0:T(8,128)(2,1)S(1)} collective-permute-done((bf16[1032,128]{1,0:T(8,128)(2,1)S(1)}, bf16[1032,128]{1,0:T(8,128)(2,1)S(1)}, u32[]{:S(2)}, u32[]{:S(2)}) %collective-permute-start.7) | collective-permute-done | bytes 264224 | tf_op jit(solution)/shard_map/ppermute | solution.py:300
  93.0 5.0 %collective-permute-done.8.rest_7_ = bf16[1032,128]{1,0:T(8,128)(2,1)S(1)} collective-permute-done((bf16[1032,128]{1,0:T(8,128)(2,1)S(1)}, bf16[1032,128]{1,0:T(8,128)(2,1)S(1)}, u32[]{:S(2)}, u32[]{:S(2)}) %collective-permute-start.8) | collective-permute-done | bytes 264224 | tf_op jit(solution)/shard_map/ppermute | solution.py:300
  98.0 3.5 %decode.3 = f32[2,2,512,1024]{3,2,1,0:T(8,128)} custom-call(bf16[1032,128]{1,0:T(8,128)(2,1)S(1)} %get-tuple-element.39.rest_0_, bf16[1032,128]{1,0:T(8,128)(2,1)S(1)} %collective-permute-done.2.rest_1_, bf16[1032,128]{1,0:T(8,128)(2,1)S(1)} %collective-permute-done.3.rest_2_, ...), custom_call_target="tpu_custom_call", output_to_operand_aliasing={{}: (8, {})} | custom-call | tf_op jit(solution)/shard_map/decode/pallas_call | solution.py:267
  (5 shorter events, 0.0 us)
Async XLA Ops:
  0.0 5.2 %slice-start = ((bf16[2,2,524288]{2,1,0:T(2,128)(2,1)}), bf16[1,2,524288]{2,1,0:T(2,128)(2,1)S(1)}, s32[]{:S(2)}) async-start(bf16[2,2,524288]{2,1,0:T(2,128)(2,1)} %param.4), calls=%async_computation | async-start | bytes 4194304 | tf_op jit(solution)/shard_map/slice | solution.py:291
  1.5 5.0 %copy-start = (f32[16,4096]{1,0:T(8,128)S(1)}, f32[16,4096]{1,0:T(8,128)}, u32[]{:S(2)}) copy-start(f32[16,4096]{1,0:T(8,128)} %taps.7) | copy-start | bytes 786436
  1.6 10.3 %collective-permute-start = (bf16[1,2,65536]{2,1,0:T(2,128)(2,1)S(1)}, bf16[1,2,65536]{2,1,0:T(2,128)(2,1)S(1)}, u32[]{:S(2)}, u32[]{:S(2)}) collective-permute-start(bf16[1,2,65536]{2,1,0:T(2,128)(2,1)S(1)} %get-tuple-element.56), channel_id=1, source_target_pairs={{0,1},{1,2},{2,3},{3,4},{4,5},{5,6},{6,7},{8,9},{9,10},{10,11},{11... | collective-permute-start | bytes 786440 | tf_op jit(solution)/shard_map/ppermute | solution.py:287
  5.2 6.8 %copy-start.1 = (bf16[256,768]{1,0:T(8,128)(2,1)S(1)}, bf16[256,768]{1,0:T(8,128)(2,1)}, u32[]{:S(2)}) copy-start(bf16[256,768]{1,0:T(8,128)(2,1)} %constant.5.clone.matrix) | copy-start | bytes 1179652
  5.2 6.8 %copy-start.2 = (f32[2,32,128]{2,1,0:T(8,128)S(1)}, f32[2,32,128]{2,1,0:T(8,128)}, u32[]{:S(2)}) copy-start(f32[2,32,128]{2,1,0:T(8,128)} %constant.4.clone.twist) | copy-start | bytes 98308
  12.0 35.7 %slice-start.1 = ((bf16[2,2,524288]{2,1,0:T(2,128)(2,1)}), bf16[1,2,524288]{2,1,0:T(2,128)(2,1)S(1)}, s32[]{:S(2)}) async-start(bf16[2,2,524288]{2,1,0:T(2,128)(2,1)} %param.4), calls=%async_computation.1 | async-start | bytes 4194304 | tf_op jit(solution)/shard_map/slice | solution.py:291
  18.0 42.2 %collective-permute-start.9 = (bf16[1032,128]{1,0:T(8,128)(2,1)S(1)}, bf16[1032,128]{1,0:T(8,128)(2,1)S(1)}, u32[]{:S(2)}, u32[]{:S(2)}) collective-permute-start(bf16[1032,128]{1,0:T(8,128)(2,1)S(1)} %get-tuple-element.48), channel_id=1, source_target_pairs={{0,1},{1,0},{2,3},{3,2},{4,5},{5,4},{6,7},{7,6},{8,9},{9,8},{10,11... | collective-permute-start | bytes 792584 | tf_op jit(solution)/shard_map/ppermute | solution.py:300
  19.5 41.9 %collective-permute-start.10 = (bf16[1032,128]{1,0:T(8,128)(2,1)S(1)}, bf16[1032,128]{1,0:T(8,128)(2,1)S(1)}, u32[]{:S(2)}, u32[]{:S(2)}) collective-permute-start(bf16[1032,128]{1,0:T(8,128)(2,1)S(1)} %get-tuple-element.49), channel_id=1, source_target_pairs={{0,2},{1,3},{2,0},{3,1},{4,6},{5,7},{6,4},{7,5},{8,10},{9,11},{10,... | collective-permute-start | bytes 792584 | tf_op jit(solution)/shard_map/ppermute | solution.py:300
  21.0 43.0 %collective-permute-start.11 = (bf16[1032,128]{1,0:T(8,128)(2,1)S(1)}, bf16[1032,128]{1,0:T(8,128)(2,1)S(1)}, u32[]{:S(2)}, u32[]{:S(2)}) collective-permute-start(bf16[1032,128]{1,0:T(8,128)(2,1)S(1)} %get-tuple-element.50), channel_id=1, source_target_pairs={{0,3},{1,2},{2,1},{3,0},{4,7},{5,6},{6,5},{7,4},{8,11},{9,10},{10,... | collective-permute-start | bytes 792584 | tf_op jit(solution)/shard_map/ppermute | solution.py:300
  21.8 43.3 %collective-permute-start.12 = (bf16[1032,128]{1,0:T(8,128)(2,1)S(1)}, bf16[1032,128]{1,0:T(8,128)(2,1)S(1)}, u32[]{:S(2)}, u32[]{:S(2)}) collective-permute-start(bf16[1032,128]{1,0:T(8,128)(2,1)S(1)} %get-tuple-element.51), channel_id=1, source_target_pairs={{0,4},{1,5},{2,6},{3,7},{4,0},{5,1},{6,2},{7,3},{8,12},{9,13},{10,... | collective-permute-start | bytes 792584 | tf_op jit(solution)/shard_map/ppermute | solution.py:300
  25.3 11.2 %collective-permute-start.1 = (bf16[1,2,65536]{2,1,0:T(2,128)(2,1)S(1)}, bf16[1,2,65536]{2,1,0:T(2,128)(2,1)S(1)}, u32[]{:S(2)}, u32[]{:S(2)}) collective-permute-start(bf16[1,2,65536]{2,1,0:T(2,128)(2,1)S(1)} %get-tuple-element.35), channel_id=1, source_target_pairs={{0,1},{1,2},{2,3},{3,4},{4,5},{5,6},{6,7},{8,9},{9,10},{10,11},{11... | collective-permute-start | bytes 786440 | tf_op jit(solution)/shard_map/ppermute | solution.py:296
  36.6 28.6 %collective-permute-start.13 = (bf16[1032,128]{1,0:T(8,128)(2,1)S(1)}, bf16[1032,128]{1,0:T(8,128)(2,1)S(1)}, u32[]{:S(2)}, u32[]{:S(2)}) collective-permute-start(bf16[1032,128]{1,0:T(8,128)(2,1)S(1)} %get-tuple-element.52), channel_id=1, source_target_pairs={{0,5},{1,4},{2,7},{3,6},{4,1},{5,0},{6,3},{7,2},{8,13},{9,12},{10,... | collective-permute-start | bytes 792584 | tf_op jit(solution)/shard_map/ppermute | solution.py:300
  60.2 8.7 %collective-permute-start.14 = (bf16[1032,128]{1,0:T(8,128)(2,1)S(1)}, bf16[1032,128]{1,0:T(8,128)(2,1)S(1)}, u32[]{:S(2)}, u32[]{:S(2)}) collective-permute-start(bf16[1032,128]{1,0:T(8,128)(2,1)S(1)} %get-tuple-element.53), channel_id=1, source_target_pairs={{0,6},{1,7},{2,4},{3,5},{4,2},{5,3},{6,0},{7,1},{8,14},{9,15},{10,... | collective-permute-start | bytes 792584 | tf_op jit(solution)/shard_map/ppermute | solution.py:300
  61.4 11.1 %collective-permute-start.15 = (bf16[1032,128]{1,0:T(8,128)(2,1)S(1)}, bf16[1032,128]{1,0:T(8,128)(2,1)S(1)}, u32[]{:S(2)}, u32[]{:S(2)}) collective-permute-start(bf16[1032,128]{1,0:T(8,128)(2,1)S(1)} %get-tuple-element.54), channel_id=1, source_target_pairs={{0,7},{1,6},{2,5},{3,4},{4,3},{5,2},{6,1},{7,0},{8,15},{9,14},{10,... | collective-permute-start | bytes 792584 | tf_op jit(solution)/shard_map/ppermute | solution.py:300
  63.9 17.0 %collective-permute-start.2 = (bf16[1032,128]{1,0:T(8,128)(2,1)S(1)}, bf16[1032,128]{1,0:T(8,128)(2,1)S(1)}, u32[]{:S(2)}, u32[]{:S(2)}) collective-permute-start(bf16[1032,128]{1,0:T(8,128)(2,1)S(1)} %get-tuple-element.40), channel_id=1, source_target_pairs={{0,1},{1,0},{2,3},{3,2},{4,5},{5,4},{6,7},{7,6},{8,9},{9,8},{10,11... | collective-permute-start | bytes 792584 | tf_op jit(solution)/shard_map/ppermute | solution.py:300
  65.0 19.8 %collective-permute-start.3 = (bf16[1032,128]{1,0:T(8,128)(2,1)S(1)}, bf16[1032,128]{1,0:T(8,128)(2,1)S(1)}, u32[]{:S(2)}, u32[]{:S(2)}) collective-permute-start(bf16[1032,128]{1,0:T(8,128)(2,1)S(1)} %get-tuple-element.41), channel_id=1, source_target_pairs={{0,2},{1,3},{2,0},{3,1},{4,6},{5,7},{6,4},{7,5},{8,10},{9,11},{10,... | collective-permute-start | bytes 792584 | tf_op jit(solution)/shard_map/ppermute | solution.py:300
  65.2 23.5 %collective-permute-start.4 = (bf16[1032,128]{1,0:T(8,128)(2,1)S(1)}, bf16[1032,128]{1,0:T(8,128)(2,1)S(1)}, u32[]{:S(2)}, u32[]{:S(2)}) collective-permute-start(bf16[1032,128]{1,0:T(8,128)(2,1)S(1)} %get-tuple-element.42), channel_id=1, source_target_pairs={{0,3},{1,2},{2,1},{3,0},{4,7},{5,6},{6,5},{7,4},{8,11},{9,10},{10,... | collective-permute-start | bytes 792584 | tf_op jit(solution)/shard_map/ppermute | solution.py:300
  68.9 19.8 %collective-permute-start.5 = (bf16[1032,128]{1,0:T(8,128)(2,1)S(1)}, bf16[1032,128]{1,0:T(8,128)(2,1)S(1)}, u32[]{:S(2)}, u32[]{:S(2)}) collective-permute-start(bf16[1032,128]{1,0:T(8,128)(2,1)S(1)} %get-tuple-element.43), channel_id=1, source_target_pairs={{0,4},{1,5},{2,6},{3,7},{4,0},{5,1},{6,2},{7,3},{8,12},{9,13},{10,... | collective-permute-start | bytes 792584 | tf_op jit(solution)/shard_map/ppermute | solution.py:300
  72.4 16.3 %collective-permute-start.6 = (bf16[1032,128]{1,0:T(8,128)(2,1)S(1)}, bf16[1032,128]{1,0:T(8,128)(2,1)S(1)}, u32[]{:S(2)}, u32[]{:S(2)}) collective-permute-start(bf16[1032,128]{1,0:T(8,128)(2,1)S(1)} %get-tuple-element.44), channel_id=1, source_target_pairs={{0,5},{1,4},{2,7},{3,6},{4,1},{5,0},{6,3},{7,2},{8,13},{9,12},{10,... | collective-permute-start | bytes 792584 | tf_op jit(solution)/shard_map/ppermute | solution.py:300
  80.9 12.0 %collective-permute-start.7 = (bf16[1032,128]{1,0:T(8,128)(2,1)S(1)}, bf16[1032,128]{1,0:T(8,128)(2,1)S(1)}, u32[]{:S(2)}, u32[]{:S(2)}) collective-permute-start(bf16[1032,128]{1,0:T(8,128)(2,1)S(1)} %get-tuple-element.45), channel_id=1, source_target_pairs={{0,6},{1,7},{2,4},{3,5},{4,2},{5,3},{6,0},{7,1},{8,14},{9,15},{10,... | collective-permute-start | bytes 792584 | tf_op jit(solution)/shard_map/ppermute | solution.py:300
  84.8 13.2 %collective-permute-start.8 = (bf16[1032,128]{1,0:T(8,128)(2,1)S(1)}, bf16[1032,128]{1,0:T(8,128)(2,1)S(1)}, u32[]{:S(2)}, u32[]{:S(2)}) collective-permute-start(bf16[1032,128]{1,0:T(8,128)(2,1)S(1)} %get-tuple-element.46), channel_id=1, source_target_pairs={{0,7},{1,6},{2,5},{3,4},{4,3},{5,2},{6,1},{7,0},{8,15},{9,14},{10,... | collective-permute-start | bytes 792584 | tf_op jit(solution)/shard_map/ppermute | solution.py:300

commit v3 on v2

--- a/solution.py
+++ b/solution.py
@@ -17,10 +17,15 @@
 PAIR = 4
 UNROLL = 4
 PITCH = 36
-ORDER = (5, 1, 4, 7, 2, 3, 6)
+ORDER = ((0, 5, 1, 4, 7, 2, 3, 6), (0, 4, 5, 1, 2, 7, 6, 3))
 POWER = 12
 FLOOR = 2.0**-10.25
 REACH = 2.0**10.25
+
+
+def partner(slot):
+    core = lax.axis_index("stream") % 2
+    return ORDER[0][slot] + core * (ORDER[1][slot] - ORDER[0][slot])
 
 
 def tables(channels):
@@ -188,7 +193,7 @@
 
     share = LANES // 8
     for d in range(8):
-        first = jnp.bitwise_xor(me, d) * share * PITCH
+        first = jnp.bitwise_xor(me, partner(d)) * share * PITCH
         for part in range(2):
             for fast in range(share):
                 start = pl.multiple_of(first + fast * PITCH, 4)
@@ -244,7 +249,7 @@
         total = jnp.sum(power, axis=1, keepdims=True)
         factor = lax.rsqrt(total / (8 * LANES) + 1.0)
         for d in range(8):
-            lanes = pl.ds(pl.multiple_of(jnp.bitwise_xor(me, d) * LANES, LANES), LANES)
+            lanes = pl.ds(pl.multiple_of(jnp.bitwise_xor(me, partner(d)) * LANES, LANES), LANES)
             for part in range(2):
                 output[0, part, pl.ds(pl.multiple_of(number * 16, 16), 16), lanes] = found[2 * d + part] * factor
         return carry
@@ -296,8 +301,13 @@
             edge = lax.ppermute(tail, "tm", route)
         pieces = list(encode(near, taps, grid, largest, twist, matrix))
         held, pieces[0] = lax.optimization_barrier((held, pieces[0]))
-        for d in ORDER:
-            pieces[d] = lax.ppermute(pieces[d], "tm", [(i, i ^ d) for i in range(size)])
+        for slot in range(1, size):
+            ways = [
+                (row * size + i, row * size + (i ^ ORDER[row % 2][slot]))
+                for row in range(lax.axis_size("stream"))
+                for i in range(size)
+            ]
+            pieces[slot] = lax.ppermute(pieces[slot], ("stream", "tm"), ways)
         arrived.append(pieces)
     output = None
     for stream in range(streams):

time: 102 us -> 95.8 us (0.939)
  starting transfers between devices: 39.5 us -> 30.5 us
  waiting for transfers between devices: 27.9 us -> 30.1 us
    ppermute x14, starting transfers between devices: 33.3 us -> 23.6 us  [shards(): pieces[slot] = lax.ppermute(pieces[slot], ('stream', 'tm'), ways)]
    ppermute x1, waiting for transfers between devices: 8.56 us -> 12 us  [shards(): edge = lax.ppermute(tail, 'tm', route)]
    ppermute x14, waiting for transfers between devices: 19.4 us -> 18 us  [shards(): pieces[slot] = lax.ppermute(pieces[slot], ('stream', 'tm'), ways)]
  transfers between devices with their start and end apart: 16 -> 16, of which waited for: 6 -> 6; matrix products, arithmetic and copies ran while one was open for 3% -> 3% of each run, Pallas kernels for 20% -> 21%
where the time goes in v3:
time: 95.8 us; the launch traced here: 94.6 us
  starting transfers between devices  30.5 us (32%)
  waiting for transfers between devices  30.1 us (31%)
  Pallas kernels  29.3 us (31%)
  local copies, waits for them, and re-layouts  4.53 us (5%)
    ppermute x14, starting transfers between devices, shards(): pieces[slot] = lax.ppermute(pieces[slot], ('stream', 'tm'), ways)  23.6 us
    ppermute x14, waiting for transfers between devices, shards(): pieces[slot] = lax.ppermute(pieces[slot], ('stream', 'tm'), ways)  18 us
    ppermute x1, waiting for transfers between devices, shards(): edge = lax.ppermute(tail, 'tm', route)  12 us
    pallas_call x2, Pallas kernels, encode(): pl.pallas_call(encode_kernel, out_shape=[piece] * 8, in_specs=[whole] * 6...  11.9 us
    pallas_call x2, Pallas kernels, filtered(): pl.pallas_call(filter_kernel, out_shape=[jax.ShapeDtypeStruct((2, SLOW, c...  10.5 us
    pallas_call x2, Pallas kernels, decode(): pl.pallas_call(decode_kernel, grid=(blocks,), out_shape=jax.ShapeDtypeStr...  6.95 us
    ppermute x1, starting transfers between devices, shards(): edge = lax.ppermute(tails[0], 'tm', route)  3.63 us
    ppermute x1, starting transfers between devices, shards(): edge = lax.ppermute(tail, 'tm', route)  3.26 us
  transfers between devices with their start and end apart: 16, of which 6 were waited for; matrix products, arithmetic and copies ran while one was open for 3% of the time, Pallas kernels for 21%

profile of v3, /device:TPU:192, one launch (start us, length us, event | category | flops | bytes accessed | tf_op | source)
XLA Modules:
  0.0 94.6 jit_solution(3636566210053287172)
XLA Ops:
  0.0 1.5 %fusion = (bf16[1,2,65536]{2,1,0:T(2,128)(2,1)S(1)}, bf16[1,2,65536]{2,1,0:T(2,128)(2,1)S(1)}) fusion(bf16[2,2,524288]{2,1,0:T(2,128)(2,1)} %param.4), kind=kLoop, calls=%fused_computation.4 | loop fusion | bytes 1048576 | tf_op jit(solution)/shard_map/slice | solution.py:291
  1.5 0.0 copy-start
  1.6 3.6 %collective-permute-start = (bf16[1,2,65536]{2,1,0:T(2,128)(2,1)S(1)}, bf16[1,2,65536]{2,1,0:T(2,128)(2,1)S(1)}, u32[]{:S(2)}, u32[]{:S(2)}) collective-permute-start(bf16[1,2,65536]{2,1,0:T(2,128)(2,1)S(1)} %get-tuple-element.56), channel_id=1, source_target_pairs={{0,1},{1,2},{2,3},{3,4},{4,5},{5,6},{6,7},{8,9},{9,10},{10,11},{11... | collective-permute-start | bytes 786440 | tf_op jit(solution)/shard_map/ppermute | solution.py:292
  5.2 0.0 copy-start.1
  5.2 0.0 copy-start.2
  5.2 1.3 %copy.15 = bf16[1,2,128,4096]{3,2,1,0:T(8,128)(2,1)S(1)} copy(bf16[1,2,128,4096]{3,1,2,0:T(2,128)(2,1)S(1)} %bitcast.24) | data formatting | bytes 4194304
  6.6 0.0 copy-done
  6.6 5.2 %filter.2 = (f32[2,32,128,128]{3,2,1,0:T(8,128)S(1)}, f32[8,128]{1,0:T(8,128)S(1)}) custom-call(bf16[2,128,4096]{2,1,0:T(8,128)(2,1)S(1)} %bitcast.20, f32[16,4096]{1,0:T(8,128)S(1)} %copy-done), custom_call_target="tpu_custom_call" | custom-call | tf_op jit(solution)/shard_map/filter/pallas_call | solution.py:104
  11.8 0.0 collective-permute-done
  11.8 0.2 copy.17
  12.0 0.0 slice-start.1
  12.0 6.0 %encode.2 = (bf16[1032,128]{1,0:T(8,128)(2,1)S(1)}, bf16[1032,128]{1,0:T(8,128)(2,1)S(1)}, bf16[1032,128]{1,0:T(8,128)(2,1)S(1)}, bf16[1032,128]{1,0:T(8,128)(2,...) custom-call(bf16[2,16,4096]{2,1,0:T(8,128)(2,1)S(1)} %bitcast.23, ...), custom_call_target="tpu_custom_call" | custom-call | tf_op jit(solution)/shard_map/encode/pallas_call | solution.py:211
  18.0 3.9 %collective-permute-start.9 = (bf16[1032,128]{1,0:T(8,128)(2,1)S(1)}, bf16[1032,128]{1,0:T(8,128)(2,1)S(1)}, u32[]{:S(2)}, u32[]{:S(2)}) collective-permute-start(bf16[1032,128]{1,0:T(8,128)(2,1)S(1)} %get-tuple-element.48), channel_id=1, source_target_pairs={{0,5},{1,4},{2,7},{3,6},{4,1},{5,0},{6,3},{7,2},{8,12},{9,13},{10,... | collective-permute-start | bytes 792584 | tf_op jit(solution)/shard_map/ppermute | solution.py:310
  21.9 1.3 %collective-permute-start.10 = (bf16[1032,128]{1,0:T(8,128)(2,1)S(1)}, bf16[1032,128]{1,0:T(8,128)(2,1)S(1)}, u32[]{:S(2)}, u32[]{:S(2)}) collective-permute-start(bf16[1032,128]{1,0:T(8,128)(2,1)S(1)} %get-tuple-element.49), channel_id=1, source_target_pairs={{0,1},{1,0},{2,3},{3,2},{4,5},{5,4},{6,7},{7,6},{8,13},{9,12},{10,... | collective-permute-start | bytes 792584 | tf_op jit(solution)/shard_map/ppermute | solution.py:310
  23.3 0.0 collective-permute-start.11
  23.3 3.4 %collective-permute-start.12 = (bf16[1032,128]{1,0:T(8,128)(2,1)S(1)}, bf16[1032,128]{1,0:T(8,128)(2,1)S(1)}, u32[]{:S(2)}, u32[]{:S(2)}) collective-permute-start(bf16[1032,128]{1,0:T(8,128)(2,1)S(1)} %get-tuple-element.51), channel_id=1, source_target_pairs={{0,7},{1,6},{2,5},{3,4},{4,3},{5,2},{6,1},{7,0},{8,10},{9,11},{10,... | collective-permute-start | bytes 792584 | tf_op jit(solution)/shard_map/ppermute | solution.py:310
  26.6 3.3 %collective-permute-start.1 = (bf16[1,2,65536]{2,1,0:T(2,128)(2,1)S(1)}, bf16[1,2,65536]{2,1,0:T(2,128)(2,1)S(1)}, u32[]{:S(2)}, u32[]{:S(2)}) collective-permute-start(bf16[1,2,65536]{2,1,0:T(2,128)(2,1)S(1)} %get-tuple-element.35), channel_id=1, source_target_pairs={{0,1},{1,2},{2,3},{3,4},{4,5},{5,6},{6,7},{8,9},{9,10},{10,11},{11... | collective-permute-start | bytes 786440 | tf_op jit(solution)/shard_map/ppermute | solution.py:301
  29.9 12.0 %collective-permute-done.1 = bf16[1,2,65536]{2,1,0:T(2,128)(2,1)S(1)} collective-permute-done((bf16[1,2,65536]{2,1,0:T(2,128)(2,1)S(1)}, bf16[1,2,65536]{2,1,0:T(2,128)(2,1)S(1)}, u32[]{:S(2)}, u32[]{:S(2)}) %collective-permute-start.1) | collective-permute-done | bytes 262176 | tf_op jit(solution)/shard_map/ppermute | solution.py:301
  42.0 0.1 copy.16
  42.1 1.7 %collective-permute-start.13 = (bf16[1032,128]{1,0:T(8,128)(2,1)S(1)}, bf16[1032,128]{1,0:T(8,128)(2,1)S(1)}, u32[]{:S(2)}, u32[]{:S(2)}) collective-permute-start(bf16[1032,128]{1,0:T(8,128)(2,1)S(1)} %get-tuple-element.52), channel_id=1, source_target_pairs={{0,2},{1,3},{2,0},{3,1},{4,6},{5,7},{6,4},{7,5},{8,15},{9,14},{10,... | collective-permute-start | bytes 792584 | tf_op jit(solution)/shard_map/ppermute | solution.py:310
  43.8 1.3 %copy.14 = bf16[1,2,128,4096]{3,2,1,0:T(8,128)(2,1)S(1)} copy(bf16[1,2,128,4096]{3,1,2,0:T(2,128)(2,1)S(1)} %bitcast.25) | data formatting | bytes 4194304
  45.1 5.2 %filter.3 = (f32[2,32,128,128]{3,2,1,0:T(8,128)S(1)}, f32[8,128]{1,0:T(8,128)S(1)}) custom-call(bf16[2,128,4096]{2,1,0:T(8,128)(2,1)S(1)} %bitcast.21, f32[16,4096]{1,0:T(8,128)S(1)} %copy-done), custom_call_target="tpu_custom_call" | custom-call | tf_op jit(solution)/shard_map/filter/pallas_call | solution.py:104
  50.4 6.0 %encode.3 = (bf16[1032,128]{1,0:T(8,128)(2,1)S(1)}, bf16[1032,128]{1,0:T(8,128)(2,1)S(1)}, bf16[1032,128]{1,0:T(8,128)(2,1)S(1)}, bf16[1032,128]{1,0:T(8,128)(2,...) custom-call(bf16[2,16,4096]{2,1,0:T(8,128)(2,1)S(1)} %bitcast.22, ...), custom_call_target="tpu_custom_call" | custom-call | tf_op jit(solution)/shard_map/encode/pallas_call | solution.py:211
  56.4 0.0 collective-permute-done.9.rest_1_
  56.4 2.4 %collective-permute-start.14 = (bf16[1032,128]{1,0:T(8,128)(2,1)S(1)}, bf16[1032,128]{1,0:T(8,128)(2,1)S(1)}, u32[]{:S(2)}, u32[]{:S(2)}) collective-permute-start(bf16[1032,128]{1,0:T(8,128)(2,1)S(1)} %get-tuple-element.53), channel_id=1, source_target_pairs={{0,3},{1,2},{2,1},{3,0},{4,7},{5,6},{6,5},{7,4},{8,14},{9,15},{10,... | collective-permute-start | bytes 792584 | tf_op jit(solution)/shard_map/ppermute | solution.py:310
  58.8 0.0 collective-permute-done.10.rest_2_
  58.8 2.9 %collective-permute-start.15 = (bf16[1032,128]{1,0:T(8,128)(2,1)S(1)}, bf16[1032,128]{1,0:T(8,128)(2,1)S(1)}, u32[]{:S(2)}, u32[]{:S(2)}) collective-permute-start(bf16[1032,128]{1,0:T(8,128)(2,1)S(1)} %get-tuple-element.54), channel_id=1, source_target_pairs={{0,6},{1,7},{2,4},{3,5},{4,2},{5,3},{6,0},{7,1},{8,11},{9,10},{10,... | collective-permute-start | bytes 792584 | tf_op jit(solution)/shard_map/ppermute | solution.py:310
  61.7 0.0 collective-permute-done.11.rest_3_
  61.7 0.0 collective-permute-start.2
  61.7 0.0 collective-permute-done.12.rest_4_
  61.7 2.3 %collective-permute-start.3 = (bf16[1032,128]{1,0:T(8,128)(2,1)S(1)}, bf16[1032,128]{1,0:T(8,128)(2,1)S(1)}, u32[]{:S(2)}, u32[]{:S(2)}) collective-permute-start(bf16[1032,128]{1,0:T(8,128)(2,1)S(1)} %get-tuple-element.41), channel_id=1, source_target_pairs={{0,1},{1,0},{2,3},{3,2},{4,5},{5,4},{6,7},{7,6},{8,13},{9,12},{10,... | collective-permute-start | bytes 792584 | tf_op jit(solution)/shard_map/ppermute | solution.py:310
  63.9 0.0 collective-permute-done.13.rest_5_
  63.9 2.7 %collective-permute-start.4 = (bf16[1032,128]{1,0:T(8,128)(2,1)S(1)}, bf16[1032,128]{1,0:T(8,128)(2,1)S(1)}, u32[]{:S(2)}, u32[]{:S(2)}) collective-permute-start(bf16[1032,128]{1,0:T(8,128)(2,1)S(1)} %get-tuple-element.42), channel_id=1, source_target_pairs={{0,4},{1,5},{2,6},{3,7},{4,0},{5,1},{6,2},{7,3},{8,9},{9,8},{10,11... | collective-permute-start | bytes 792584 | tf_op jit(solution)/shard_map/ppermute | solution.py:310
  66.7 0.0 collective-permute-done.14.rest_6_
  66.7 2.9 %collective-permute-start.5 = (bf16[1032,128]{1,0:T(8,128)(2,1)S(1)}, bf16[1032,128]{1,0:T(8,128)(2,1)S(1)}, u32[]{:S(2)}, u32[]{:S(2)}) collective-permute-start(bf16[1032,128]{1,0:T(8,128)(2,1)S(1)} %get-tuple-element.43), channel_id=1, source_target_pairs={{0,7},{1,6},{2,5},{3,4},{4,3},{5,2},{6,1},{7,0},{8,10},{9,11},{10,... | collective-permute-start | bytes 792584 | tf_op jit(solution)/shard_map/ppermute | solution.py:310
  69.5 10.2 %collective-permute-done.15.rest_7_ = bf16[1032,128]{1,0:T(8,128)(2,1)S(1)} collective-permute-done((bf16[1032,128]{1,0:T(8,128)(2,1)S(1)}, bf16[1032,128]{1,0:T(8,128)(2,1)S(1)}, u32[]{:S(2)}, u32[]{:S(2)}) %collective-permute-start.15) | collective-permute-done | bytes 264224 | tf_op jit(solution)/shard_map/ppermute | solution.py:310
  79.8 0.0 collective-permute-start.6
  79.8 0.0 collective-permute-done.2.rest_1_
  79.8 0.0 collective-permute-start.7
  79.8 0.0 collective-permute-done.3.rest_2_
  79.8 0.1 collective-permute-start.8
  79.9 3.5 %decode.2.rest_8_ = f32[2,2,512,1024]{3,2,1,0:T(8,128)} custom-call(bf16[1032,128]{1,0:T(8,128)(2,1)S(1)} %get-tuple-element.47.rest_0_, bf16[1032,128]{1,0:T(8,128)(2,1)S(1)} %collective-permute-done.9.rest_1_, bf16[1032,128]{1,0:T(8,128)(2,1)S(1)} %collective-permute-done.10.rest_2_, bf16[1032,128]{1,0:T(8,128)(2,1)S(1)} %collective-permute-done.11.rest_3_, ...), custom_call_target="tpu_custom_call" | custom-call | tf_op jit(solution)/shard_map/decode/pallas_call | solution.py:272
  83.4 0.0 collective-permute-done.4.rest_3_
  83.4 3.2 %collective-permute-done.5.rest_4_ = bf16[1032,128]{1,0:T(8,128)(2,1)S(1)} collective-permute-done((bf16[1032,128]{1,0:T(8,128)(2,1)S(1)}, bf16[1032,128]{1,0:T(8,128)(2,1)S(1)}, u32[]{:S(2)}, u32[]{:S(2)}) %collective-permute-start.5) | collective-permute-done | bytes 264224 | tf_op jit(solution)/shard_map/ppermute | solution.py:310
  86.6 2.4 %collective-permute-done.6.rest_5_ = bf16[1032,128]{1,0:T(8,128)(2,1)S(1)} collective-permute-done((bf16[1032,128]{1,0:T(8,128)(2,1)S(1)}, bf16[1032,128]{1,0:T(8,128)(2,1)S(1)}, u32[]{:S(2)}, u32[]{:S(2)}) %collective-permute-start.6) | collective-permute-done | bytes 264224 | tf_op jit(solution)/shard_map/ppermute | solution.py:310
  89.0 1.9 %collective-permute-done.7.rest_6_ = bf16[1032,128]{1,0:T(8,128)(2,1)S(1)} collective-permute-done((bf16[1032,128]{1,0:T(8,128)(2,1)S(1)}, bf16[1032,128]{1,0:T(8,128)(2,1)S(1)}, u32[]{:S(2)}, u32[]{:S(2)}) %collective-permute-start.7) | collective-permute-done | bytes 264224 | tf_op jit(solution)/shard_map/ppermute | solution.py:310
  91.0 0.2 collective-permute-done.8.rest_7_
  91.2 3.5 %decode.3 = f32[2,2,512,1024]{3,2,1,0:T(8,128)} custom-call(bf16[1032,128]{1,0:T(8,128)(2,1)S(1)} %get-tuple-element.39.rest_0_, bf16[1032,128]{1,0:T(8,128)(2,1)S(1)} %collective-permute-done.2.rest_1_, bf16[1032,128]{1,0:T(8,128)(2,1)S(1)} %collective-permute-done.3.rest_2_, ...), custom_call_target="tpu_custom_call", output_to_operand_aliasing={{}: (8, {})} | custom-call | tf_op jit(solution)/shard_map/decode/pallas_call | solution.py:272
  (5 shorter events, 0.0 us)
Async XLA Ops:
  0.0 5.2 %slice-start = ((bf16[2,2,524288]{2,1,0:T(2,128)(2,1)}), bf16[1,2,524288]{2,1,0:T(2,128)(2,1)S(1)}, s32[]{:S(2)}) async-start(bf16[2,2,524288]{2,1,0:T(2,128)(2,1)} %param.4), calls=%async_computation | async-start | bytes 4194304 | tf_op jit(solution)/shard_map/slice | solution.py:296
  1.5 5.0 %copy-start = (f32[16,4096]{1,0:T(8,128)S(1)}, f32[16,4096]{1,0:T(8,128)}, u32[]{:S(2)}) copy-start(f32[16,4096]{1,0:T(8,128)} %taps.7) | copy-start | bytes 786436
  1.6 10.3 %collective-permute-start = (bf16[1,2,65536]{2,1,0:T(2,128)(2,1)S(1)}, bf16[1,2,65536]{2,1,0:T(2,128)(2,1)S(1)}, u32[]{:S(2)}, u32[]{:S(2)}) collective-permute-start(bf16[1,2,65536]{2,1,0:T(2,128)(2,1)S(1)} %get-tuple-element.56), channel_id=1, source_target_pairs={{0,1},{1,2},{2,3},{3,4},{4,5},{5,6},{6,7},{8,9},{9,10},{10,11},{11... | collective-permute-start | bytes 786440 | tf_op jit(solution)/shard_map/ppermute | solution.py:292
  5.2 6.8 %copy-start.1 = (bf16[256,768]{1,0:T(8,128)(2,1)S(1)}, bf16[256,768]{1,0:T(8,128)(2,1)}, u32[]{:S(2)}) copy-start(bf16[256,768]{1,0:T(8,128)(2,1)} %constant.5.clone.matrix) | copy-start | bytes 1179652
  5.2 6.8 %copy-start.2 = (f32[2,32,128]{2,1,0:T(8,128)S(1)}, f32[2,32,128]{2,1,0:T(8,128)}, u32[]{:S(2)}) copy-start(f32[2,32,128]{2,1,0:T(8,128)} %constant.4.clone.twist) | copy-start | bytes 98308
  12.0 31.8 %slice-start.1 = ((bf16[2,2,524288]{2,1,0:T(2,128)(2,1)}), bf16[1,2,524288]{2,1,0:T(2,128)(2,1)S(1)}, s32[]{:S(2)}) async-start(bf16[2,2,524288]{2,1,0:T(2,128)(2,1)} %param.4), calls=%async_computation.1 | async-start | bytes 4194304 | tf_op jit(solution)/shard_map/slice | solution.py:296
  18.0 38.4 %collective-permute-start.9 = (bf16[1032,128]{1,0:T(8,128)(2,1)S(1)}, bf16[1032,128]{1,0:T(8,128)(2,1)S(1)}, u32[]{:S(2)}, u32[]{:S(2)}) collective-permute-start(bf16[1032,128]{1,0:T(8,128)(2,1)S(1)} %get-tuple-element.48), channel_id=1, source_target_pairs={{0,5},{1,4},{2,7},{3,6},{4,1},{5,0},{6,3},{7,2},{8,12},{9,13},{10,... | collective-permute-start | bytes 792584 | tf_op jit(solution)/shard_map/ppermute | solution.py:310
  21.9 36.9 %collective-permute-start.10 = (bf16[1032,128]{1,0:T(8,128)(2,1)S(1)}, bf16[1032,128]{1,0:T(8,128)(2,1)S(1)}, u32[]{:S(2)}, u32[]{:S(2)}) collective-permute-start(bf16[1032,128]{1,0:T(8,128)(2,1)S(1)} %get-tuple-element.49), channel_id=1, source_target_pairs={{0,1},{1,0},{2,3},{3,2},{4,5},{5,4},{6,7},{7,6},{8,13},{9,12},{10,... | collective-permute-start | bytes 792584 | tf_op jit(solution)/shard_map/ppermute | solution.py:310
  23.3 38.4 %collective-permute-start.11 = (bf16[1032,128]{1,0:T(8,128)(2,1)S(1)}, bf16[1032,128]{1,0:T(8,128)(2,1)S(1)}, u32[]{:S(2)}, u32[]{:S(2)}) collective-permute-start(bf16[1032,128]{1,0:T(8,128)(2,1)S(1)} %get-tuple-element.50), channel_id=1, source_target_pairs={{0,4},{1,5},{2,6},{3,7},{4,0},{5,1},{6,2},{7,3},{8,9},{9,8},{10,11... | collective-permute-start | bytes 792584 | tf_op jit(solution)/shard_map/ppermute | solution.py:310
  23.3 38.4 %collective-permute-start.12 = (bf16[1032,128]{1,0:T(8,128)(2,1)S(1)}, bf16[1032,128]{1,0:T(8,128)(2,1)S(1)}, u32[]{:S(2)}, u32[]{:S(2)}) collective-permute-start(bf16[1032,128]{1,0:T(8,128)(2,1)S(1)} %get-tuple-element.51), channel_id=1, source_target_pairs={{0,7},{1,6},{2,5},{3,4},{4,3},{5,2},{6,1},{7,0},{8,10},{9,11},{10,... | collective-permute-start | bytes 792584 | tf_op jit(solution)/shard_map/ppermute | solution.py:310
  26.6 15.3 %collective-permute-start.1 = (bf16[1,2,65536]{2,1,0:T(2,128)(2,1)S(1)}, bf16[1,2,65536]{2,1,0:T(2,128)(2,1)S(1)}, u32[]{:S(2)}, u32[]{:S(2)}) collective-permute-start(bf16[1,2,65536]{2,1,0:T(2,128)(2,1)S(1)} %get-tuple-element.35), channel_id=1, source_target_pairs={{0,1},{1,2},{2,3},{3,4},{4,5},{5,6},{6,7},{8,9},{9,10},{10,11},{11... | collective-permute-start | bytes 786440 | tf_op jit(solution)/shard_map/ppermute | solution.py:301
  42.1 21.8 %collective-permute-start.13 = (bf16[1032,128]{1,0:T(8,128)(2,1)S(1)}, bf16[1032,128]{1,0:T(8,128)(2,1)S(1)}, u32[]{:S(2)}, u32[]{:S(2)}) collective-permute-start(bf16[1032,128]{1,0:T(8,128)(2,1)S(1)} %get-tuple-element.52), channel_id=1, source_target_pairs={{0,2},{1,3},{2,0},{3,1},{4,6},{5,7},{6,4},{7,5},{8,15},{9,14},{10,... | collective-permute-start | bytes 792584 | tf_op jit(solution)/shard_map/ppermute | solution.py:310
  56.4 10.3 %collective-permute-start.14 = (bf16[1032,128]{1,0:T(8,128)(2,1)S(1)}, bf16[1032,128]{1,0:T(8,128)(2,1)S(1)}, u32[]{:S(2)}, u32[]{:S(2)}) collective-permute-start(bf16[1032,128]{1,0:T(8,128)(2,1)S(1)} %get-tuple-element.53), channel_id=1, source_target_pairs={{0,3},{1,2},{2,1},{3,0},{4,7},{5,6},{6,5},{7,4},{8,14},{9,15},{10,... | collective-permute-start | bytes 792584 | tf_op jit(solution)/shard_map/ppermute | solution.py:310
  58.8 21.0 %collective-permute-start.15 = (bf16[1032,128]{1,0:T(8,128)(2,1)S(1)}, bf16[1032,128]{1,0:T(8,128)(2,1)S(1)}, u32[]{:S(2)}, u32[]{:S(2)}) collective-permute-start(bf16[1032,128]{1,0:T(8,128)(2,1)S(1)} %get-tuple-element.54), channel_id=1, source_target_pairs={{0,6},{1,7},{2,4},{3,5},{4,2},{5,3},{6,0},{7,1},{8,11},{9,10},{10,... | collective-permute-start | bytes 792584 | tf_op jit(solution)/shard_map/ppermute | solution.py:310
  61.7 18.1 %collective-permute-start.2 = (bf16[1032,128]{1,0:T(8,128)(2,1)S(1)}, bf16[1032,128]{1,0:T(8,128)(2,1)S(1)}, u32[]{:S(2)}, u32[]{:S(2)}) collective-permute-start(bf16[1032,128]{1,0:T(8,128)(2,1)S(1)} %get-tuple-element.40), channel_id=1, source_target_pairs={{0,5},{1,4},{2,7},{3,6},{4,1},{5,0},{6,3},{7,2},{8,12},{9,13},{10,... | collective-permute-start | bytes 792584 | tf_op jit(solution)/shard_map/ppermute | solution.py:310
  61.7 18.1 %collective-permute-start.3 = (bf16[1032,128]{1,0:T(8,128)(2,1)S(1)}, bf16[1032,128]{1,0:T(8,128)(2,1)S(1)}, u32[]{:S(2)}, u32[]{:S(2)}) collective-permute-start(bf16[1032,128]{1,0:T(8,128)(2,1)S(1)} %get-tuple-element.41), channel_id=1, source_target_pairs={{0,1},{1,0},{2,3},{3,2},{4,5},{5,4},{6,7},{7,6},{8,13},{9,12},{10,... | collective-permute-start | bytes 792584 | tf_op jit(solution)/shard_map/ppermute | solution.py:310
  63.9 19.5 %collective-permute-start.4 = (bf16[1032,128]{1,0:T(8,128)(2,1)S(1)}, bf16[1032,128]{1,0:T(8,128)(2,1)S(1)}, u32[]{:S(2)}, u32[]{:S(2)}) collective-permute-start(bf16[1032,128]{1,0:T(8,128)(2,1)S(1)} %get-tuple-element.42), channel_id=1, source_target_pairs={{0,4},{1,5},{2,6},{3,7},{4,0},{5,1},{6,2},{7,3},{8,9},{9,8},{10,11... | collective-permute-start | bytes 792584 | tf_op jit(solution)/shard_map/ppermute | solution.py:310
  66.7 19.9 %collective-permute-start.5 = (bf16[1032,128]{1,0:T(8,128)(2,1)S(1)}, bf16[1032,128]{1,0:T(8,128)(2,1)S(1)}, u32[]{:S(2)}, u32[]{:S(2)}) collective-permute-start(bf16[1032,128]{1,0:T(8,128)(2,1)S(1)} %get-tuple-element.43), channel_id=1, source_target_pairs={{0,7},{1,6},{2,5},{3,4},{4,3},{5,2},{6,1},{7,0},{8,10},{9,11},{10,... | collective-permute-start | bytes 792584 | tf_op jit(solution)/shard_map/ppermute | solution.py:310
  79.8 9.2 %collective-permute-start.6 = (bf16[1032,128]{1,0:T(8,128)(2,1)S(1)}, bf16[1032,128]{1,0:T(8,128)(2,1)S(1)}, u32[]{:S(2)}, u32[]{:S(2)}) collective-permute-start(bf16[1032,128]{1,0:T(8,128)(2,1)S(1)} %get-tuple-element.44), channel_id=1, source_target_pairs={{0,2},{1,3},{2,0},{3,1},{4,6},{5,7},{6,4},{7,5},{8,15},{9,14},{10,... | collective-permute-start | bytes 792584 | tf_op jit(solution)/shard_map/ppermute | solution.py:310
  79.8 11.2 %collective-permute-start.7 = (bf16[1032,128]{1,0:T(8,128)(2,1)S(1)}, bf16[1032,128]{1,0:T(8,128)(2,1)S(1)}, u32[]{:S(2)}, u32[]{:S(2)}) collective-permute-start(bf16[1032,128]{1,0:T(8,128)(2,1)S(1)} %get-tuple-element.45), channel_id=1, source_target_pairs={{0,3},{1,2},{2,1},{3,0},{4,7},{5,6},{6,5},{7,4},{8,14},{9,15},{10,... | collective-permute-start | bytes 792584 | tf_op jit(solution)/shard_map/ppermute | solution.py:310
  79.8 11.3 %collective-permute-start.8 = (bf16[1032,128]{1,0:T(8,128)(2,1)S(1)}, bf16[1032,128]{1,0:T(8,128)(2,1)S(1)}, u32[]{:S(2)}, u32[]{:S(2)}) collective-permute-start(bf16[1032,128]{1,0:T(8,128)(2,1)S(1)} %get-tuple-element.46), channel_id=1, source_target_pairs={{0,6},{1,7},{2,4},{3,5},{4,2},{5,3},{6,0},{7,1},{8,11},{9,10},{10,... | collective-permute-start | bytes 792584 | tf_op jit(solution)/shard_map/ppermute | solution.py:310

commit v4 on v2

--- a/solution.py
+++ b/solution.py
@@ -15,9 +15,9 @@
 TURN = 16
 LEAD = 16
 PAIR = 4
-UNROLL = 4
+UNROLL = 8
 PITCH = 36
-ORDER = (5, 1, 4, 7, 2, 3, 6)
+ORDER = (1, 5, 4, 7, 2, 3, 6)
 POWER = 12
 FLOOR = 2.0**-10.25
 REACH = 2.0**10.25
@@ -116,24 +116,23 @@
     depth = taps.shape[0]
     count = grid.shape[2]
     me = lax.axis_index("tm")
-    window[pl.ds(LEAD, LEAD), :] = jnp.zeros((LEAD, LANES), jnp.float32)
-
-    def head_step(number, most):
-        part = number // SLOW
-        slow = number % SLOW
+    window[:, pl.ds(LEAD, LEAD), :] = jnp.zeros((2, LEAD, LANES), jnp.float32)
+
+    def head_step(slow, most):
         columns = pl.ds(pl.multiple_of(slow * LANES, LANES), LANES)
-        window[pl.ds(0, LEAD), :] = edge[part, :, columns].astype(jnp.float32)
         weights = [taps[pl.ds(k, 1), columns] for k in range(depth)]
-        for block in range(LEAD // 8):
-            times = pl.ds(block * 8, 8)
-            total = grid[part, slow, times, :]
-            for k in range(8 * block + 1, depth):
-                total = total + weights[k] * window[pl.ds(LEAD + block * 8 - k, 8), :]
-            head[part, slow, times, :] = total
-            most = jnp.maximum(most, jnp.abs(total))
+        for part in range(2):
+            window[part, pl.ds(0, LEAD), :] = edge[part, :, columns].astype(jnp.float32)
+            for block in range(LEAD // 8):
+                times = pl.ds(block * 8, 8)
+                total = grid[part, slow, times, :]
+                for k in range(8 * block + 1, depth):
+                    total = total + weights[k] * window[part, pl.ds(LEAD + block * 8 - k, 8), :]
+                head[part, slow, times, :] = total
+                most = jnp.maximum(most, jnp.abs(total))
         return most
 
-    most = lax.fori_loop(0, 2 * SLOW, head_step, largest[...], unroll=4)
+    most = lax.fori_loop(0, SLOW, head_step, largest[...], unroll=4)
     bound = jnp.max(most) * math.sqrt(2.0 * LANES * SLOW)
     scale = jnp.full((8, LANES), REACH, jnp.float32) / jnp.maximum(bound, 1e-35)
     scale = scale.astype(jnp.bfloat16).astype(jnp.float32)
@@ -209,7 +208,7 @@
         in_specs=[whole] * 6,
         out_specs=[whole] * 8,
         scratch_shapes=[
-            pltpu.VMEM((2 * LEAD, LANES), jnp.float32),
+            pltpu.VMEM((2, 2 * LEAD, LANES), jnp.float32),
             pltpu.VMEM((2, SLOW, LEAD, LANES), jnp.float32),
             pltpu.VMEM((2, SLOW, TURN, LANES), jnp.float32),
             pltpu.VMEM((SLOW, count, 2 * LANES), jnp.bfloat16),

time: 102 us -> 101 us (level)
  Pallas kernels: 29.4 us -> 28.1 us
    pallas_call x2, Pallas kernels: 12 us -> 10.7 us  [encode(): pl.pallas_call(encode_kernel, out_shape=[piece] * 8, in_specs=[whole] * 6...]
  transfers between devices with their start and end apart: 16 -> 16, of which waited for: 6 -> 7; matrix products, arithmetic and copies ran while one was open for 3% -> 3% of each run, Pallas kernels for 20% -> 19%
where the time goes in v4:
time: 101 us
  starting transfers between devices  39.4 us (39%)
  waiting for transfers between devices  28.4 us (28%)
  Pallas kernels  28.1 us (28%)
  local copies, waits for them, and re-layouts  4.53 us (4%)
    ppermute x14, starting transfers between devices, shards(): pieces[d] = lax.ppermute(pieces[d], 'tm', [(i, i ^ d) for i in range(size)])  33.2 us
    ppermute x14, waiting for transfers between devices, shards(): pieces[d] = lax.ppermute(pieces[d], 'tm', [(i, i ^ d) for i in range(size)])  19.8 us
    pallas_call x2, Pallas kernels, encode(): pl.pallas_call(encode_kernel, out_shape=[piece] * 8, in_specs=[whole] * 6...  10.7 us
    pallas_call x2, Pallas kernels, filtered(): pl.pallas_call(filter_kernel, out_shape=[jax.ShapeDtypeStruct((2, SLOW, c...  10.5 us
    ppermute x1, waiting for transfers between devices, shards(): edge = lax.ppermute(tail, 'tm', route)  8.56 us
    pallas_call x2, Pallas kernels, decode(): pl.pallas_call(decode_kernel, grid=(blocks,), out_shape=jax.ShapeDtypeStr...  6.93 us
    ppermute x1, starting transfers between devices, shards(): edge = lax.ppermute(tails[0], 'tm', route)  3.63 us
    unnamed x10, local copies, waits for them, and re-layouts  2.98 us
  transfers between devices with their start and end apart: 16, of which 7 were waited for; matrix products, arithmetic and copies ran while one was open for 3% of the time, Pallas kernels for 19%

profile of v4, /device:TPU:192, one launch (start us, length us, event | category | flops | bytes accessed | tf_op | source)
XLA Modules:
  0.0 100.6 jit_solution(10316635325433491395)
XLA Ops:
  0.0 1.5 %fusion = (bf16[1,2,65536]{2,1,0:T(2,128)(2,1)S(1)}, bf16[1,2,65536]{2,1,0:T(2,128)(2,1)S(1)}) fusion(bf16[2,2,524288]{2,1,0:T(2,128)(2,1)} %param.4), kind=kLoop, calls=%fused_computation.4 | loop fusion | bytes 1048576 | tf_op jit(solution)/shard_map/slice | solution.py:285
  1.5 0.0 copy-start
  1.6 3.6 %collective-permute-start = (bf16[1,2,65536]{2,1,0:T(2,128)(2,1)S(1)}, bf16[1,2,65536]{2,1,0:T(2,128)(2,1)S(1)}, u32[]{:S(2)}, u32[]{:S(2)}) collective-permute-start(bf16[1,2,65536]{2,1,0:T(2,128)(2,1)S(1)} %get-tuple-element.56), channel_id=1, source_target_pairs={{0,1},{1,2},{2,3},{3,4},{4,5},{5,6},{6,7},{8,9},{9,10},{10,11},{11... | collective-permute-start | bytes 786440 | tf_op jit(solution)/shard_map/ppermute | solution.py:286
  5.2 0.0 copy-start.1
  5.2 0.0 copy-start.2
  5.2 1.3 %copy.15 = bf16[1,2,128,4096]{3,2,1,0:T(8,128)(2,1)S(1)} copy(bf16[1,2,128,4096]{3,1,2,0:T(2,128)(2,1)S(1)} %bitcast.24) | data formatting | bytes 4194304
  6.6 0.0 copy-done
  6.6 5.2 %filter.2 = (f32[2,32,128,128]{3,2,1,0:T(8,128)S(1)}, f32[8,128]{1,0:T(8,128)S(1)}) custom-call(bf16[2,128,4096]{2,1,0:T(8,128)(2,1)S(1)} %bitcast.20, f32[16,4096]{1,0:T(8,128)S(1)} %copy-done), custom_call_target="tpu_custom_call" | custom-call | tf_op jit(solution)/shard_map/filter/pallas_call | solution.py:99
  11.8 0.0 collective-permute-done
  11.8 0.2 copy.17
  12.0 0.0 slice-start.1
  12.0 5.4 %encode.2 = (bf16[1032,128]{1,0:T(8,128)(2,1)S(1)}, bf16[1032,128]{1,0:T(8,128)(2,1)S(1)}, bf16[1032,128]{1,0:T(8,128)(2,1)S(1)}, bf16[1032,128]{1,0:T(8,128)(2,...) custom-call(bf16[2,16,4096]{2,1,0:T(8,128)(2,1)S(1)} %bitcast.23, ...), custom_call_target="tpu_custom_call" | custom-call | tf_op jit(solution)/shard_map/encode/pallas_call | solution.py:205
  17.4 1.5 %collective-permute-start.9 = (bf16[1032,128]{1,0:T(8,128)(2,1)S(1)}, bf16[1032,128]{1,0:T(8,128)(2,1)S(1)}, u32[]{:S(2)}, u32[]{:S(2)}) collective-permute-start(bf16[1032,128]{1,0:T(8,128)(2,1)S(1)} %get-tuple-element.48), channel_id=1, source_target_pairs={{0,1},{1,0},{2,3},{3,2},{4,5},{5,4},{6,7},{7,6},{8,9},{9,8},{10,11... | collective-permute-start | bytes 792584 | tf_op jit(solution)/shard_map/ppermute | solution.py:299
  18.8 1.5 %collective-permute-start.10 = (bf16[1032,128]{1,0:T(8,128)(2,1)S(1)}, bf16[1032,128]{1,0:T(8,128)(2,1)S(1)}, u32[]{:S(2)}, u32[]{:S(2)}) collective-permute-start(bf16[1032,128]{1,0:T(8,128)(2,1)S(1)} %get-tuple-element.49), channel_id=1, source_target_pairs={{0,2},{1,3},{2,0},{3,1},{4,6},{5,7},{6,4},{7,5},{8,10},{9,11},{10,... | collective-permute-start | bytes 792584 | tf_op jit(solution)/shard_map/ppermute | solution.py:299
  20.3 0.8 collective-permute-start.11
  21.1 3.6 %collective-permute-start.12 = (bf16[1032,128]{1,0:T(8,128)(2,1)S(1)}, bf16[1032,128]{1,0:T(8,128)(2,1)S(1)}, u32[]{:S(2)}, u32[]{:S(2)}) collective-permute-start(bf16[1032,128]{1,0:T(8,128)(2,1)S(1)} %get-tuple-element.51), channel_id=1, source_target_pairs={{0,4},{1,5},{2,6},{3,7},{4,0},{5,1},{6,2},{7,3},{8,12},{9,13},{10,... | collective-permute-start | bytes 792584 | tf_op jit(solution)/shard_map/ppermute | solution.py:299
  24.7 2.6 %collective-permute-start.1 = (bf16[1,2,65536]{2,1,0:T(2,128)(2,1)S(1)}, bf16[1,2,65536]{2,1,0:T(2,128)(2,1)S(1)}, u32[]{:S(2)}, u32[]{:S(2)}) collective-permute-start(bf16[1,2,65536]{2,1,0:T(2,128)(2,1)S(1)} %get-tuple-element.35), channel_id=1, source_target_pairs={{0,1},{1,2},{2,3},{3,4},{4,5},{5,6},{6,7},{8,9},{9,10},{10,11},{11... | collective-permute-start | bytes 786440 | tf_op jit(solution)/shard_map/ppermute | solution.py:295
  27.3 8.6 %collective-permute-done.1 = bf16[1,2,65536]{2,1,0:T(2,128)(2,1)S(1)} collective-permute-done((bf16[1,2,65536]{2,1,0:T(2,128)(2,1)S(1)}, bf16[1,2,65536]{2,1,0:T(2,128)(2,1)S(1)}, u32[]{:S(2)}, u32[]{:S(2)}) %collective-permute-start.1) | collective-permute-done | bytes 262176 | tf_op jit(solution)/shard_map/ppermute | solution.py:295
  35.8 0.1 copy.16
  36.0 11.0 %collective-permute-start.13 = (bf16[1032,128]{1,0:T(8,128)(2,1)S(1)}, bf16[1032,128]{1,0:T(8,128)(2,1)S(1)}, u32[]{:S(2)}, u32[]{:S(2)}) collective-permute-start(bf16[1032,128]{1,0:T(8,128)(2,1)S(1)} %get-tuple-element.52), channel_id=1, source_target_pairs={{0,5},{1,4},{2,7},{3,6},{4,1},{5,0},{6,3},{7,2},{8,13},{9,12},{10,... | collective-permute-start | bytes 792584 | tf_op jit(solution)/shard_map/ppermute | solution.py:299
  47.0 1.3 %copy.14 = bf16[1,2,128,4096]{3,2,1,0:T(8,128)(2,1)S(1)} copy(bf16[1,2,128,4096]{3,1,2,0:T(2,128)(2,1)S(1)} %bitcast.25) | data formatting | bytes 4194304
  48.3 5.2 %filter.3 = (f32[2,32,128,128]{3,2,1,0:T(8,128)S(1)}, f32[8,128]{1,0:T(8,128)S(1)}) custom-call(bf16[2,128,4096]{2,1,0:T(8,128)(2,1)S(1)} %bitcast.21, f32[16,4096]{1,0:T(8,128)S(1)} %copy-done), custom_call_target="tpu_custom_call" | custom-call | tf_op jit(solution)/shard_map/filter/pallas_call | solution.py:99
  53.6 5.4 %encode.3 = (bf16[1032,128]{1,0:T(8,128)(2,1)S(1)}, bf16[1032,128]{1,0:T(8,128)(2,1)S(1)}, bf16[1032,128]{1,0:T(8,128)(2,1)S(1)}, bf16[1032,128]{1,0:T(8,128)(2,...) custom-call(bf16[2,16,4096]{2,1,0:T(8,128)(2,1)S(1)} %bitcast.22, ...), custom_call_target="tpu_custom_call" | custom-call | tf_op jit(solution)/shard_map/encode/pallas_call | solution.py:205
  58.9 0.0 collective-permute-done.9.rest_1_
  59.0 1.1 %collective-permute-start.14 = (bf16[1032,128]{1,0:T(8,128)(2,1)S(1)}, bf16[1032,128]{1,0:T(8,128)(2,1)S(1)}, u32[]{:S(2)}, u32[]{:S(2)}) collective-permute-start(bf16[1032,128]{1,0:T(8,128)(2,1)S(1)} %get-tuple-element.53), channel_id=1, source_target_pairs={{0,6},{1,7},{2,4},{3,5},{4,2},{5,3},{6,0},{7,1},{8,14},{9,15},{10,... | collective-permute-start | bytes 792584 | tf_op jit(solution)/shard_map/ppermute | solution.py:299
  60.1 0.0 collective-permute-done.10.rest_2_
  60.1 2.4 %collective-permute-start.15 = (bf16[1032,128]{1,0:T(8,128)(2,1)S(1)}, bf16[1032,128]{1,0:T(8,128)(2,1)S(1)}, u32[]{:S(2)}, u32[]{:S(2)}) collective-permute-start(bf16[1032,128]{1,0:T(8,128)(2,1)S(1)} %get-tuple-element.54), channel_id=1, source_target_pairs={{0,7},{1,6},{2,5},{3,4},{4,3},{5,2},{6,1},{7,0},{8,15},{9,14},{10,... | collective-permute-start | bytes 792584 | tf_op jit(solution)/shard_map/ppermute | solution.py:299
  62.5 0.0 collective-permute-done.11.rest_3_
  62.5 1.3 %collective-permute-start.2 = (bf16[1032,128]{1,0:T(8,128)(2,1)S(1)}, bf16[1032,128]{1,0:T(8,128)(2,1)S(1)}, u32[]{:S(2)}, u32[]{:S(2)}) collective-permute-start(bf16[1032,128]{1,0:T(8,128)(2,1)S(1)} %get-tuple-element.40), channel_id=1, source_target_pairs={{0,1},{1,0},{2,3},{3,2},{4,5},{5,4},{6,7},{7,6},{8,9},{9,8},{10,11... | collective-permute-start | bytes 792584 | tf_op jit(solution)/shard_map/ppermute | solution.py:299
  63.7 0.0 collective-permute-done.12.rest_4_
  63.7 0.2 collective-permute-start.3
  63.9 0.0 collective-permute-done.13.rest_5_
  64.0 2.0 %collective-permute-start.4 = (bf16[1032,128]{1,0:T(8,128)(2,1)S(1)}, bf16[1032,128]{1,0:T(8,128)(2,1)S(1)}, u32[]{:S(2)}, u32[]{:S(2)}) collective-permute-start(bf16[1032,128]{1,0:T(8,128)(2,1)S(1)} %get-tuple-element.42), channel_id=1, source_target_pairs={{0,3},{1,2},{2,1},{3,0},{4,7},{5,6},{6,5},{7,4},{8,11},{9,10},{10,... | collective-permute-start | bytes 792584 | tf_op jit(solution)/shard_map/ppermute | solution.py:299
  66.0 1.8 %collective-permute-done.14.rest_6_ = bf16[1032,128]{1,0:T(8,128)(2,1)S(1)} collective-permute-done((bf16[1032,128]{1,0:T(8,128)(2,1)S(1)}, bf16[1032,128]{1,0:T(8,128)(2,1)S(1)}, u32[]{:S(2)}, u32[]{:S(2)}) %collective-permute-start.14) | collective-permute-done | bytes 264224 | tf_op jit(solution)/shard_map/ppermute | solution.py:299
  67.8 0.8 collective-permute-start.5
  68.6 2.8 %collective-permute-done.15.rest_7_ = bf16[1032,128]{1,0:T(8,128)(2,1)S(1)} collective-permute-done((bf16[1032,128]{1,0:T(8,128)(2,1)S(1)}, bf16[1032,128]{1,0:T(8,128)(2,1)S(1)}, u32[]{:S(2)}, u32[]{:S(2)}) %collective-permute-start.15) | collective-permute-done | bytes 264224 | tf_op jit(solution)/shard_map/ppermute | solution.py:299
  71.4 2.3 %collective-permute-start.6 = (bf16[1032,128]{1,0:T(8,128)(2,1)S(1)}, bf16[1032,128]{1,0:T(8,128)(2,1)S(1)}, u32[]{:S(2)}, u32[]{:S(2)}) collective-permute-start(bf16[1032,128]{1,0:T(8,128)(2,1)S(1)} %get-tuple-element.44), channel_id=1, source_target_pairs={{0,5},{1,4},{2,7},{3,6},{4,1},{5,0},{6,3},{7,2},{8,13},{9,12},{10,... | collective-permute-start | bytes 792584 | tf_op jit(solution)/shard_map/ppermute | solution.py:299
  73.7 5.4 %collective-permute-done.2.rest_1_ = bf16[1032,128]{1,0:T(8,128)(2,1)S(1)} collective-permute-done((bf16[1032,128]{1,0:T(8,128)(2,1)S(1)}, bf16[1032,128]{1,0:T(8,128)(2,1)S(1)}, u32[]{:S(2)}, u32[]{:S(2)}) %collective-permute-start.2) | collective-permute-done | bytes 264224 | tf_op jit(solution)/shard_map/ppermute | solution.py:299
  79.1 4.6 %collective-permute-start.7 = (bf16[1032,128]{1,0:T(8,128)(2,1)S(1)}, bf16[1032,128]{1,0:T(8,128)(2,1)S(1)}, u32[]{:S(2)}, u32[]{:S(2)}) collective-permute-start(bf16[1032,128]{1,0:T(8,128)(2,1)S(1)} %get-tuple-element.45), channel_id=1, source_target_pairs={{0,6},{1,7},{2,4},{3,5},{4,2},{5,3},{6,0},{7,1},{8,14},{9,15},{10,... | collective-permute-start | bytes 792584 | tf_op jit(solution)/shard_map/ppermute | solution.py:299
  83.7 0.0 collective-permute-done.3.rest_2_
  83.7 0.0 collective-permute-start.8
  83.7 3.5 %decode.2.rest_8_ = f32[2,2,512,1024]{3,2,1,0:T(8,128)} custom-call(bf16[1032,128]{1,0:T(8,128)(2,1)S(1)} %get-tuple-element.47.rest_0_, bf16[1032,128]{1,0:T(8,128)(2,1)S(1)} %collective-permute-done.9.rest_1_, bf16[1032,128]{1,0:T(8,128)(2,1)S(1)} %collective-permute-done.10.rest_2_, bf16[1032,128]{1,0:T(8,128)(2,1)S(1)} %collective-permute-done.11.rest_3_, ...), custom_call_target="tpu_custom_call" | custom-call | tf_op jit(solution)/shard_map/decode/pallas_call | solution.py:266
  87.2 0.0 collective-permute-done.4.rest_3_
  87.2 0.0 collective-permute-done.5.rest_4_
  87.2 0.5 collective-permute-done.6.rest_5_
  87.8 4.2 %collective-permute-done.7.rest_6_ = bf16[1032,128]{1,0:T(8,128)(2,1)S(1)} collective-permute-done((bf16[1032,128]{1,0:T(8,128)(2,1)S(1)}, bf16[1032,128]{1,0:T(8,128)(2,1)S(1)}, u32[]{:S(2)}, u32[]{:S(2)}) %collective-permute-start.7) | collective-permute-done | bytes 264224 | tf_op jit(solution)/shard_map/ppermute | solution.py:299
  92.0 5.1 %collective-permute-done.8.rest_7_ = bf16[1032,128]{1,0:T(8,128)(2,1)S(1)} collective-permute-done((bf16[1032,128]{1,0:T(8,128)(2,1)S(1)}, bf16[1032,128]{1,0:T(8,128)(2,1)S(1)}, u32[]{:S(2)}, u32[]{:S(2)}) %collective-permute-start.8) | collective-permute-done | bytes 264224 | tf_op jit(solution)/shard_map/ppermute | solution.py:299
  97.1 3.5 %decode.3 = f32[2,2,512,1024]{3,2,1,0:T(8,128)} custom-call(bf16[1032,128]{1,0:T(8,128)(2,1)S(1)} %get-tuple-element.39.rest_0_, bf16[1032,128]{1,0:T(8,128)(2,1)S(1)} %collective-permute-done.2.rest_1_, bf16[1032,128]{1,0:T(8,128)(2,1)S(1)} %collective-permute-done.3.rest_2_, ...), custom_call_target="tpu_custom_call", output_to_operand_aliasing={{}: (8, {})} | custom-call | tf_op jit(solution)/shard_map/decode/pallas_call | solution.py:266
  (5 shorter events, 0.0 us)
Async XLA Ops:
  0.0 5.2 %slice-start = ((bf16[2,2,524288]{2,1,0:T(2,128)(2,1)}), bf16[1,2,524288]{2,1,0:T(2,128)(2,1)S(1)}, s32[]{:S(2)}) async-start(bf16[2,2,524288]{2,1,0:T(2,128)(2,1)} %param.4), calls=%async_computation | async-start | bytes 4194304 | tf_op jit(solution)/shard_map/slice | solution.py:290
  1.5 5.0 %copy-start = (f32[16,4096]{1,0:T(8,128)S(1)}, f32[16,4096]{1,0:T(8,128)}, u32[]{:S(2)}) copy-start(f32[16,4096]{1,0:T(8,128)} %taps.7) | copy-start | bytes 786436
  1.6 10.3 %collective-permute-start = (bf16[1,2,65536]{2,1,0:T(2,128)(2,1)S(1)}, bf16[1,2,65536]{2,1,0:T(2,128)(2,1)S(1)}, u32[]{:S(2)}, u32[]{:S(2)}) collective-permute-start(bf16[1,2,65536]{2,1,0:T(2,128)(2,1)S(1)} %get-tuple-element.56), channel_id=1, source_target_pairs={{0,1},{1,2},{2,3},{3,4},{4,5},{5,6},{6,7},{8,9},{9,10},{10,11},{11... | collective-permute-start | bytes 786440 | tf_op jit(solution)/shard_map/ppermute | solution.py:286
  5.2 6.8 %copy-start.1 = (bf16[256,768]{1,0:T(8,128)(2,1)S(1)}, bf16[256,768]{1,0:T(8,128)(2,1)}, u32[]{:S(2)}) copy-start(bf16[256,768]{1,0:T(8,128)(2,1)} %constant.5.clone.matrix) | copy-start | bytes 1179652
  5.2 6.8 %copy-start.2 = (f32[2,32,128]{2,1,0:T(8,128)S(1)}, f32[2,32,128]{2,1,0:T(8,128)}, u32[]{:S(2)}) copy-start(f32[2,32,128]{2,1,0:T(8,128)} %constant.4.clone.twist) | copy-start | bytes 98308
  12.0 35.0 %slice-start.1 = ((bf16[2,2,524288]{2,1,0:T(2,128)(2,1)}), bf16[1,2,524288]{2,1,0:T(2,128)(2,1)S(1)}, s32[]{:S(2)}) async-start(bf16[2,2,524288]{2,1,0:T(2,128)(2,1)} %param.4), calls=%async_computation.1 | async-start | bytes 4194304 | tf_op jit(solution)/shard_map/slice | solution.py:290
  17.4 41.6 %collective-permute-start.9 = (bf16[1032,128]{1,0:T(8,128)(2,1)S(1)}, bf16[1032,128]{1,0:T(8,128)(2,1)S(1)}, u32[]{:S(2)}, u32[]{:S(2)}) collective-permute-start(bf16[1032,128]{1,0:T(8,128)(2,1)S(1)} %get-tuple-element.48), channel_id=1, source_target_pairs={{0,1},{1,0},{2,3},{3,2},{4,5},{5,4},{6,7},{7,6},{8,9},{9,8},{10,11... | collective-permute-start | bytes 792584 | tf_op jit(solution)/shard_map/ppermute | solution.py:299
  18.8 41.3 %collective-permute-start.10 = (bf16[1032,128]{1,0:T(8,128)(2,1)S(1)}, bf16[1032,128]{1,0:T(8,128)(2,1)S(1)}, u32[]{:S(2)}, u32[]{:S(2)}) collective-permute-start(bf16[1032,128]{1,0:T(8,128)(2,1)S(1)} %get-tuple-element.49), channel_id=1, source_target_pairs={{0,2},{1,3},{2,0},{3,1},{4,6},{5,7},{6,4},{7,5},{8,10},{9,11},{10,... | collective-permute-start | bytes 792584 | tf_op jit(solution)/shard_map/ppermute | solution.py:299
  20.3 42.2 %collective-permute-start.11 = (bf16[1032,128]{1,0:T(8,128)(2,1)S(1)}, bf16[1032,128]{1,0:T(8,128)(2,1)S(1)}, u32[]{:S(2)}, u32[]{:S(2)}) collective-permute-start(bf16[1032,128]{1,0:T(8,128)(2,1)S(1)} %get-tuple-element.50), channel_id=1, source_target_pairs={{0,3},{1,2},{2,1},{3,0},{4,7},{5,6},{6,5},{7,4},{8,11},{9,10},{10,... | collective-permute-start | bytes 792584 | tf_op jit(solution)/shard_map/ppermute | solution.py:299
  21.1 42.6 %collective-permute-start.12 = (bf16[1032,128]{1,0:T(8,128)(2,1)S(1)}, bf16[1032,128]{1,0:T(8,128)(2,1)S(1)}, u32[]{:S(2)}, u32[]{:S(2)}) collective-permute-start(bf16[1032,128]{1,0:T(8,128)(2,1)S(1)} %get-tuple-element.51), channel_id=1, source_target_pairs={{0,4},{1,5},{2,6},{3,7},{4,0},{5,1},{6,2},{7,3},{8,12},{9,13},{10,... | collective-permute-start | bytes 792584 | tf_op jit(solution)/shard_map/ppermute | solution.py:299
  24.7 11.2 %collective-permute-start.1 = (bf16[1,2,65536]{2,1,0:T(2,128)(2,1)S(1)}, bf16[1,2,65536]{2,1,0:T(2,128)(2,1)S(1)}, u32[]{:S(2)}, u32[]{:S(2)}) collective-permute-start(bf16[1,2,65536]{2,1,0:T(2,128)(2,1)S(1)} %get-tuple-element.35), channel_id=1, source_target_pairs={{0,1},{1,2},{2,3},{3,4},{4,5},{5,6},{6,7},{8,9},{9,10},{10,11},{11... | collective-permute-start | bytes 786440 | tf_op jit(solution)/shard_map/ppermute | solution.py:295
  36.0 28.0 %collective-permute-start.13 = (bf16[1032,128]{1,0:T(8,128)(2,1)S(1)}, bf16[1032,128]{1,0:T(8,128)(2,1)S(1)}, u32[]{:S(2)}, u32[]{:S(2)}) collective-permute-start(bf16[1032,128]{1,0:T(8,128)(2,1)S(1)} %get-tuple-element.52), channel_id=1, source_target_pairs={{0,5},{1,4},{2,7},{3,6},{4,1},{5,0},{6,3},{7,2},{8,13},{9,12},{10,... | collective-permute-start | bytes 792584 | tf_op jit(solution)/shard_map/ppermute | solution.py:299
  59.0 8.8 %collective-permute-start.14 = (bf16[1032,128]{1,0:T(8,128)(2,1)S(1)}, bf16[1032,128]{1,0:T(8,128)(2,1)S(1)}, u32[]{:S(2)}, u32[]{:S(2)}) collective-permute-start(bf16[1032,128]{1,0:T(8,128)(2,1)S(1)} %get-tuple-element.53), channel_id=1, source_target_pairs={{0,6},{1,7},{2,4},{3,5},{4,2},{5,3},{6,0},{7,1},{8,14},{9,15},{10,... | collective-permute-start | bytes 792584 | tf_op jit(solution)/shard_map/ppermute | solution.py:299
  60.1 11.3 %collective-permute-start.15 = (bf16[1032,128]{1,0:T(8,128)(2,1)S(1)}, bf16[1032,128]{1,0:T(8,128)(2,1)S(1)}, u32[]{:S(2)}, u32[]{:S(2)}) collective-permute-start(bf16[1032,128]{1,0:T(8,128)(2,1)S(1)} %get-tuple-element.54), channel_id=1, source_target_pairs={{0,7},{1,6},{2,5},{3,4},{4,3},{5,2},{6,1},{7,0},{8,15},{9,14},{10,... | collective-permute-start | bytes 792584 | tf_op jit(solution)/shard_map/ppermute | solution.py:299
  62.5 16.6 %collective-permute-start.2 = (bf16[1032,128]{1,0:T(8,128)(2,1)S(1)}, bf16[1032,128]{1,0:T(8,128)(2,1)S(1)}, u32[]{:S(2)}, u32[]{:S(2)}) collective-permute-start(bf16[1032,128]{1,0:T(8,128)(2,1)S(1)} %get-tuple-element.40), channel_id=1, source_target_pairs={{0,1},{1,0},{2,3},{3,2},{4,5},{5,4},{6,7},{7,6},{8,9},{9,8},{10,11... | collective-permute-start | bytes 792584 | tf_op jit(solution)/shard_map/ppermute | solution.py:299
  63.7 20.0 %collective-permute-start.3 = (bf16[1032,128]{1,0:T(8,128)(2,1)S(1)}, bf16[1032,128]{1,0:T(8,128)(2,1)S(1)}, u32[]{:S(2)}, u32[]{:S(2)}) collective-permute-start(bf16[1032,128]{1,0:T(8,128)(2,1)S(1)} %get-tuple-element.41), channel_id=1, source_target_pairs={{0,2},{1,3},{2,0},{3,1},{4,6},{5,7},{6,4},{7,5},{8,10},{9,11},{10,... | collective-permute-start | bytes 792584 | tf_op jit(solution)/shard_map/ppermute | solution.py:299
  64.0 23.3 %collective-permute-start.4 = (bf16[1032,128]{1,0:T(8,128)(2,1)S(1)}, bf16[1032,128]{1,0:T(8,128)(2,1)S(1)}, u32[]{:S(2)}, u32[]{:S(2)}) collective-permute-start(bf16[1032,128]{1,0:T(8,128)(2,1)S(1)} %get-tuple-element.42), channel_id=1, source_target_pairs={{0,3},{1,2},{2,1},{3,0},{4,7},{5,6},{6,5},{7,4},{8,11},{9,10},{10,... | collective-permute-start | bytes 792584 | tf_op jit(solution)/shard_map/ppermute | solution.py:299
  67.8 19.4 %collective-permute-start.5 = (bf16[1032,128]{1,0:T(8,128)(2,1)S(1)}, bf16[1032,128]{1,0:T(8,128)(2,1)S(1)}, u32[]{:S(2)}, u32[]{:S(2)}) collective-permute-start(bf16[1032,128]{1,0:T(8,128)(2,1)S(1)} %get-tuple-element.43), channel_id=1, source_target_pairs={{0,4},{1,5},{2,6},{3,7},{4,0},{5,1},{6,2},{7,3},{8,12},{9,13},{10,... | collective-permute-start | bytes 792584 | tf_op jit(solution)/shard_map/ppermute | solution.py:299
  71.4 16.4 %collective-permute-start.6 = (bf16[1032,128]{1,0:T(8,128)(2,1)S(1)}, bf16[1032,128]{1,0:T(8,128)(2,1)S(1)}, u32[]{:S(2)}, u32[]{:S(2)}) collective-permute-start(bf16[1032,128]{1,0:T(8,128)(2,1)S(1)} %get-tuple-element.44), channel_id=1, source_target_pairs={{0,5},{1,4},{2,7},{3,6},{4,1},{5,0},{6,3},{7,2},{8,13},{9,12},{10,... | collective-permute-start | bytes 792584 | tf_op jit(solution)/shard_map/ppermute | solution.py:299
  79.1 12.9 %collective-permute-start.7 = (bf16[1032,128]{1,0:T(8,128)(2,1)S(1)}, bf16[1032,128]{1,0:T(8,128)(2,1)S(1)}, u32[]{:S(2)}, u32[]{:S(2)}) collective-permute-start(bf16[1032,128]{1,0:T(8,128)(2,1)S(1)} %get-tuple-element.45), channel_id=1, source_target_pairs={{0,6},{1,7},{2,4},{3,5},{4,2},{5,3},{6,0},{7,1},{8,14},{9,15},{10,... | collective-permute-start | bytes 792584 | tf_op jit(solution)/shard_map/ppermute | solution.py:299
  83.7 13.4 %collective-permute-start.8 = (bf16[1032,128]{1,0:T(8,128)(2,1)S(1)}, bf16[1032,128]{1,0:T(8,128)(2,1)S(1)}, u32[]{:S(2)}, u32[]{:S(2)}) collective-permute-start(bf16[1032,128]{1,0:T(8,128)(2,1)S(1)} %get-tuple-element.46), channel_id=1, source_target_pairs={{0,7},{1,6},{2,5},{3,4},{4,3},{5,2},{6,1},{7,0},{8,15},{9,14},{10,... | collective-permute-start | bytes 792584 | tf_op jit(solution)/shard_map/ppermute | solution.py:299
